TPU v7x, 32 devices: a whole 2x2x4 slice. The times are simulated.
32 devices in a mesh: groups: 2 (over x), tp: 16 (over z, y, core).
Axes of the slice: x: 2, y: 2, z: 4, core: 2. Of those that a mesh axis runs over, the one named last changes fastest.
Arguments:
- queries: bfloat16 [4, 4096, 4096], P('groups', 'tp'), parts along dimension 0, may hold values from -162 to 162
- keys: bfloat16 [4, 4096, 2048], P('groups', 'tp'), parts along dimension 0, may hold values from -6 to 6
- values: bfloat16 [4, 4096, 2048], P('groups', 'tp'), parts along dimension 0, may hold values from -6 to 6
- lengths: int32 [4], P('groups'), parts along dimension 0, may hold values from 1024 to 4096
Outputs:
- attended: bfloat16 [4, 4096, 4096], P('groups', 'tp'), parts along dimension 0
There are 2 independent parts, one for each index of `groups`. A program takes and returns all parts, laid end to end along the dimension named above; each array names one. Nothing has to cross between parts.
All inputs are finite; a program needn't handle non-finite values.
Results may differ from a plain program's by a relative error of at most 0.0085.
Values may be sent and summed in bfloat16 or wider, within the bound.
A program may use at most 256 MiB of HBM per device.

v0:
```python
import jax
import jax.numpy as jnp
from jax import lax
from jax.sharding import PartitionSpec as P

HEADS = 32
KVH = 16
HD = 128


query_scale = 144.0 ** (-0.5)
soft_cap = 50.0


def block_attend(block_q, start, key_rows, value_rows, valid):
    width = block_q.shape[1]
    count = key_rows.shape[1]
    score = (
        jnp.einsum("gqd,gkd->gqk", block_q, key_rows, preferred_element_type=jnp.float32)
        * query_scale
    )
    capped = soft_cap * jnp.tanh(score / soft_cap)
    query_pos = start + jnp.arange(width)
    key_pos = jnp.arange(count)
    allowed = (key_pos[None, None, :] <= query_pos[None, :, None]) & (
        key_pos[None, None, :] < valid[:, None, None]
    )
    weight = jnp.where(allowed, jnp.exp(capped), 0.0)
    total = jnp.sum(weight, axis=2)
    mixed = jnp.einsum(
        "gqk,gkd->gqd", weight.astype(jnp.bfloat16), value_rows, preferred_element_type=jnp.float32
    )
    mixed = mixed / total[:, :, None]
    live = query_pos[None, :] < valid[:, None]
    return jnp.where(live[:, :, None], mixed, 0.0).astype(jnp.bfloat16)


def attend_all(local_q, local_k, local_v, valid):
    items, length, depth = local_q.shape
    width = min(512, length)
    blocks = length // width
    pieces = []
    for index in range(blocks):
        block_q = local_q[:, index * width : (index + 1) * width]
        upper = (index + 1) * width
        pieces.append(
            block_attend(block_q, index * width, local_k[:, :upper], local_v[:, :upper], valid)
        )
    return jnp.concatenate(pieces, axis=1)


def per_device(queries, keys, values, lengths):
    seqs, rows, _ = queries.shape
    devices = lax.axis_size("tp")
    pairs = seqs * HEADS
    owned = pairs // devices
    heads_q = queries.reshape(seqs, rows, HEADS, HD).transpose(0, 2, 1, 3).reshape(pairs, rows, HD)
    heads_k = keys.reshape(seqs, rows, KVH, HD).transpose(0, 2, 1, 3)
    heads_v = values.reshape(seqs, rows, KVH, HD).transpose(0, 2, 1, 3)
    copy_k = jnp.repeat(heads_k, 2, axis=1).reshape(pairs, rows, HD)
    copy_v = jnp.repeat(heads_v, 2, axis=1).reshape(pairs, rows, HD)
    local_q, local_k, local_v = (
        lax.all_to_all(heads_q, "tp", split_axis=0, concat_axis=1, tiled=True),
        lax.all_to_all(copy_k, "tp", split_axis=0, concat_axis=1, tiled=True),
        lax.all_to_all(copy_v, "tp", split_axis=0, concat_axis=1, tiled=True),
    )
    pair_ids = lax.axis_index("tp") * owned + jnp.arange(owned, dtype=jnp.int32)
    seq_ids = pair_ids // HEADS
    matches = seq_ids[:, None] == jnp.arange(seqs, dtype=jnp.int32)[None, :]
    valid = jnp.sum(jnp.where(matches, lengths[None, :], 0), axis=1)
    output = attend_all(local_q, local_k, local_v, valid)
    returned = lax.all_to_all(output, "tp", split_axis=1, concat_axis=0, tiled=True)
    return (
        returned.reshape(seqs, HEADS, rows, HD)
        .transpose(0, 2, 1, 3)
        .reshape(seqs, rows, HEADS * HD)
    )


def solution(mesh):
    placed = (
        P("groups", "tp", None),
        P("groups", "tp", None),
        P("groups", "tp", None),
        P("groups"),
    )
    return jax.shard_map(
        per_device, mesh=mesh, in_specs=placed, out_specs=P("groups", "tp", None), check_vma=False
    )
```

profile of v0, /device:TPU:1, one launch (start us, length us, event | category | flops | bytes accessed | tf_op | source)
XLA Modules:
  0.0 596.2 jit_solution(6410805941139451146)
XLA Ops:
  0.0 2.2 copy.64
  2.6 0.5 copy.53
  3.1 3.0 broadcast_in_dim.174
  6.2 7.3 %all-to-all-start.1 = ((bf16[64,256,128]{2,1,0:T(8,128)(2,1)}), bf16[64,256,128]{2,1,0:T(8,128)(2,1)}, u32[]{:S(2)}, u32[]{:S(2)}) async-start(bf16[64,256,128]{2,1,0:T(8,128)(2,1)} %bitcast.45), calls=%async_computation.1 | async-start | bytes 8388608 | tf_op jit(solution)/shard_map/all_to_all | solution.py:64
  13.5 6.4 %copy.50 = bf16[2,256,4096]{1,2,0:T(8,128)(2,1)} copy(bf16[2,256,4096]{2,1,0:T(8,128)(2,1)} %param.4) | data formatting | bytes 8388608 | tf_op args[0]
  19.9 6.3 %copy.51 = bf16[2,32,256,128]{3,2,1,0:T(8,128)(2,1)} copy(bf16[2,32,256,128]{2,3,1,0:T(8,128)(2,1)} %bitcast.49) | data formatting | bytes 8388608 | tf_op jit(solution)/shard_map/transpose | solution.py:57
  26.2 65.4 %all-to-all-done.1 = bf16[64,256,128]{2,1,0:T(8,128)(2,1)} async-done(((bf16[64,256,128]{2,1,0:T(8,128)(2,1)}), bf16[64,256,128]{2,1,0:T(8,128)(2,1)}, u32[]{:S(2)}, u32[]{:S(2)}) %all-to-all-start.1) | async-done | bytes 4194336 | tf_op jit(solution)/shard_map/all_to_all | solution.py:64
  91.6 19.2 %all-to-all-start = ((bf16[64,256,128]{2,1,0:T(8,128)(2,1)}), bf16[64,256,128]{2,1,0:T(8,128)(2,1)}, u32[]{:S(2)}, u32[]{:S(2)}) async-start(bf16[64,256,128]{2,1,0:T(8,128)(2,1)} %bitcast.43), calls=%async_computation | async-start | bytes 8388608 | tf_op jit(solution)/shard_map/all_to_all | solution.py:63
  110.9 0.6 copy.65
  111.9 0.5 copy.55
  112.7 0.7 broadcast_compare_fusion
  113.4 1.2 iota_compare_fusion.6
  114.6 74.4 %all-to-all-done = bf16[64,256,128]{2,1,0:T(8,128)(2,1)} async-done(((bf16[64,256,128]{2,1,0:T(8,128)(2,1)}), bf16[64,256,128]{2,1,0:T(8,128)(2,1)}, u32[]{:S(2)}, u32[]{:S(2)}) %all-to-all-start) | async-done | bytes 4194336 | tf_op jit(solution)/shard_map/all_to_all | solution.py:63
  189.0 2.9 broadcast_in_dim.176
  192.0 19.5 %all-to-all-start.2 = ((bf16[64,256,128]{2,1,0:T(8,128)(2,1)}), bf16[64,256,128]{2,1,0:T(8,128)(2,1)}, u32[]{:S(2)}, u32[]{:S(2)}) async-start(bf16[64,256,128]{2,1,0:T(8,128)(2,1)} %bitcast.44), calls=%async_computation.2 | async-start | bytes 8388608 | tf_op jit(solution)/shard_map/all_to_all | solution.py:65
  211.5 0.8 iota_compare_fusion.7
  212.9 1.6 iota_compare_fusion.4
  214.7 1.9 iota_compare_fusion.3
  216.6 2.4 iota_compare_fusion.2
  219.2 2.7 iota_compare_fusion.1
  221.8 3.0 iota_compare_fusion
  224.9 4.7 copy.54
  229.6 4.6 copy.52
  234.2 55.3 %all-to-all-done.2 = bf16[64,256,128]{2,1,0:T(8,128)(2,1)} async-done(((bf16[64,256,128]{2,1,0:T(8,128)(2,1)}), bf16[64,256,128]{2,1,0:T(8,128)(2,1)}, u32[]{:S(2)}, u32[]{:S(2)}) %all-to-all-start.2) | async-done | bytes 4194336 | tf_op jit(solution)/shard_map/all_to_all | solution.py:65
  289.5 2.8 copy.56
  292.3 0.6 copy-done.1
  292.9 2.8 copy-done.2
  295.7 4.1 fusion.48
  299.8 4.9 fusion.36
  304.7 7.9 %fusion.30 = (f32[4,512]{1,0:T(4,128)S(1)}, f32[4,512,1536]{2,1,0:T(8,128)}) fusion(pred[4,1536]{1,0:T(4,128)(4,1)S(1)} %iota_compare_fusion.13, pred[512,1536]{1,0:T(8,128)(4,1)S(1)} %iota_compare_fusion.5, bf16[4,4096,128]{2,1,0:T(8,128)(2,1)S(1)} %bitcast.63, bf16[4,4096,128]{2,1,0:T(8,128)(2,1)S(1)} %bitcast.72), kind=kOutput, calls=%fused_computation.33 | convolution fusion | flops 821032960 | bytes 15480832 | tf_op jit(solution)/shard_map/gqd,gkd->gqk/dot_general | solution.py:19
  312.6 9.5 %fusion.20 = (f32[4,512]{1,0:T(4,128)S(1)}, f32[4,512,2048]{2,1,0:T(8,128)}) fusion(pred[4,2048]{1,0:T(4,128)(4,1)S(1)} %iota_compare_fusion.12, pred[512,2048]{1,0:T(8,128)(4,1)S(1)} %copy-done.9, bf16[4,4096,128]{2,1,0:T(8,128)(2,1)S(1)} %bitcast.64, bf16[4,4096,128]{2,1,0:T(8,128)(2,1)S(1)} %bitcast.73), kind=kOutput, calls=%fused_computation.23 | convolution fusion | flops 1094711296 | bytes 20463616 | tf_op jit(solution)/shard_map/gqd,gkd->gqk/dot_general | solution.py:19
  322.1 10.7 %fusion.14 = (f32[4,512]{1,0:T(4,128)S(1)}, f32[4,512,2560]{2,1,0:T(8,128)}) fusion(pred[4,2560]{1,0:T(4,128)(4,1)S(1)} %iota_compare_fusion.11, pred[512,2560]{1,0:T(8,128)(4,1)S(1)} %copy-done.7, bf16[4,4096,128]{2,1,0:T(8,128)(2,1)S(1)} %bitcast.65, bf16[4,4096,128]{2,1,0:T(8,128)(2,1)S(1)} %bitcast.74), kind=kOutput, calls=%fused_computation.17 | convolution fusion | flops 1368389632 | bytes 25446400 | tf_op jit(solution)/shard_map/gqd,gkd->gqk/dot_general | solution.py:19
  332.8 12.2 %fusion.8 = (f32[4,512]{1,0:T(4,128)S(1)}, f32[4,512,3072]{2,1,0:T(8,128)}) fusion(pred[4,3072]{1,0:T(4,128)(4,1)S(1)} %iota_compare_fusion.10, pred[512,3072]{1,0:T(8,128)(4,1)S(1)} %copy-done.5, bf16[4,4096,128]{2,1,0:T(8,128)(2,1)S(1)} %bitcast.66, bf16[4,4096,128]{2,1,0:T(8,128)(2,1)S(1)} %bitcast.75), kind=kOutput, calls=%fused_computation.12 | convolution fusion | flops 1642067968 | bytes 30429184 | tf_op jit(solution)/shard_map/gqd,gkd->gqk/dot_general | solution.py:19
  345.1 15.2 %fusion.2 = (f32[4,512]{1,0:T(4,128)S(1)}, f32[4,512,3584]{2,1,0:T(8,128)}) fusion(pred[4,3584]{1,0:T(4,128)(4,1)S(1)} %iota_compare_fusion.9, pred[512,3584]{1,0:T(8,128)(4,1)S(1)} %copy-done.4, bf16[4,4096,128]{2,1,0:T(8,128)(2,1)S(1)} %bitcast.67, bf16[4,4096,128]{2,1,0:T(8,128)(2,1)} %bitcast.68), kind=kOutput, calls=%fused_computation.6 | convolution fusion | flops 1915746304 | bytes 35411968 | tf_op jit(solution)/shard_map/gqd,gkd->gqk/dot_general | solution.py:19
  360.3 19.6 %fusion = (f32[4,512]{1,0:T(4,128)S(1)}, f32[4,512,4096]{2,1,0:T(8,128)}) fusion(pred[4,4096]{1,0:T(4,128)(4,1)S(1)} %iota_compare_fusion.8, pred[512,4096]{1,0:T(8,128)(4,1)} %iota_compare_fusion, bf16[4,4096,128]{2,1,0:T(8,128)(2,1)} %bitcast.60, bf16[4,4096,128]{2,1,0:T(8,128)(2,1)} %bitcast.69), kind=kOutput, calls=%fused_computation.3 | convolution fusion | flops 2189424640 | bytes 40394752 | tf_op jit(solution)/shard_map/gqd,gkd->gqk/dot_general | solution.py:19
  379.9 4.7 fusion.118
  384.6 6.1 %fusion.75 = bf16[4,4096,128]{2,1,0:T(8,128)(2,1)} fusion(bf16[4,4096,128]{2,1,0:T(8,128)(2,1)} %fusion.118, bf16[4,4096,128]{2,1,0:T(8,128)(2,1)S(1)} %bitcast.53, f32[4,512,1024]{2,1,0:T(8,128)} %get-tuple-element.16, pred[4,1024]{1,0:T(4,128)(4,1)S(1)} %iota_compare_fusion.14, pred[512,1024]{1,0:T(8,128)(4,1)S(1)} %copy-done.12, ...), kind=kOutput, calls=%fused_computation.85 | convolution fusion | flops 548143104 | bytes 10500096 | tf_op jit(solution)/shard_map/gqk,gkd->gqd/dot_general | solution.py:30
  390.8 4.4 fusion.84
  395.2 9.5 %fusion.93 = bf16[4,4096,128]{2,1,0:T(8,128)(2,1)} fusion(bf16[4,4096,128]{2,1,0:T(8,128)(2,1)} %fusion.84, bf16[4,4096,128]{2,1,0:T(8,128)(2,1)S(1)} %bitcast.55, f32[4,512,2048]{2,1,0:T(8,128)} %get-tuple-element.20, pred[4,2048]{1,0:T(4,128)(4,1)S(1)} %iota_compare_fusion.12, pred[512,2048]{1,0:T(8,128)(4,1)S(1)} %copy-done.10, ...), kind=kOutput, calls=%fused_computation.87 | convolution fusion | flops 1095499776 | bytes 20465664 | tf_op jit(solution)/shard_map/gqk,gkd->gqd/dot_general | solution.py:30
  404.7 11.4 %fusion.102 = bf16[4,4096,128]{2,1,0:T(8,128)(2,1)} fusion(bf16[4,4096,128]{2,1,0:T(8,128)(2,1)} %fusion.93, bf16[4,4096,128]{2,1,0:T(8,128)(2,1)S(1)} %bitcast.56, f32[4,512,2560]{2,1,0:T(8,128)} %get-tuple-element.22, pred[4,2560]{1,0:T(4,128)(4,1)S(1)} %iota_compare_fusion.11, pred[512,2560]{1,0:T(8,128)(4,1)S(1)} %copy-done.8, ...), kind=kOutput, calls=%fused_computation.88 | convolution fusion | flops 1369178112 | bytes 25448448 | tf_op jit(solution)/shard_map/gqk,gkd->gqd/dot_general | solution.py:30
  416.1 13.6 %fusion.111 = bf16[4,4096,128]{2,1,0:T(8,128)(2,1)} fusion(bf16[4,4096,128]{2,1,0:T(8,128)(2,1)} %fusion.102, bf16[4,4096,128]{2,1,0:T(8,128)(2,1)S(1)} %bitcast.57, f32[4,512,3072]{2,1,0:T(8,128)} %get-tuple-element.24, pred[4,3072]{1,0:T(4,128)(4,1)S(1)} %iota_compare_fusion.10, pred[512,3072]{1,0:T(8,128)(4,1)S(1)} %copy-done.6, ...), kind=kOutput, calls=%fused_computation.89 | convolution fusion | flops 1642856448 | bytes 30431232 | tf_op jit(solution)/shard_map/gqk,gkd->gqd/dot_general | solution.py:30
  429.7 15.2 %fusion.125 = bf16[4,4096,128]{2,1,0:T(8,128)(2,1)} fusion(bf16[4,4096,128]{2,1,0:T(8,128)(2,1)} %fusion.111, bf16[4,4096,128]{2,1,0:T(8,128)(2,1)S(1)} %bitcast.58, f32[4,512,3584]{2,1,0:T(8,128)} %get-tuple-element.26, pred[4,3584]{1,0:T(4,128)(4,1)S(1)} %iota_compare_fusion.9, pred[512,3584]{1,0:T(8,128)(4,1)} %iota_compare_fusion.1, ...), kind=kOutput, calls=%fused_computation.91 | convolution fusion | flops 1916534784 | bytes 35414016 | tf_op jit(solution)/shard_map/gqk,gkd->gqd/dot_general | solution.py:30
  444.9 18.3 %fusion.68 = bf16[4,4096,128]{2,1,0:T(8,128)(2,1)} fusion(bf16[4,4096,128]{2,1,0:T(8,128)(2,1)} %fusion.125, bf16[4,4096,128]{2,1,0:T(8,128)(2,1)} %bitcast.59, f32[4,512,4096]{2,1,0:T(8,128)} %get-tuple-element.28, pred[4,4096]{1,0:T(4,128)(4,1)S(1)} %iota_compare_fusion.8, pred[512,4096]{1,0:T(8,128)(4,1)} %iota_compare_fusion, ...), kind=kOutput, calls=%fused_computation.84 | convolution fusion | flops 2190213120 | bytes 40396800 | tf_op jit(solution)/shard_map/gqk,gkd->gqd/dot_general | solution.py:30
  463.2 5.8 copy.58
  469.0 111.5 %all_to_all.69 = bf16[4,4096,128]{2,0,1:T(4,128)(2,1)S(1)} all-to-all(bf16[4,4096,128]{2,0,1:T(4,128)(2,1)S(1)} %copy.58), channel_id=1, replica_groups=mesh['groups'=2,'tp'=16] {'tp'}, dimensions={1} | all-to-all | bytes 8388608 | tf_op jit(solution)/shard_map/all_to_all | solution.py:72
  581.0 2.3 copy.60
  583.3 6.3 %copy.61 = bf16[2,256,32,128]{1,3,2,0:T(8,128)(2,1)} copy(bf16[2,256,32,128]{3,1,2,0:T(8,128)(2,1)} %bitcast.47) | data formatting | bytes 8388608 | tf_op jit(solution)/shard_map/transpose | solution.py:75
  589.7 6.3 %copy.62 = bf16[2,256,4096]{2,1,0:T(8,128)(2,1)} copy(bf16[2,256,4096]{1,2,0:T(8,128)(2,1)} %bitcast.48) | data formatting | bytes 8388608 | tf_op jit(solution)/shard_map/reshape | solution.py:76
  (58 shorter events, 2.5 us)
Async XLA Ops:
  6.2 85.5 %all-to-all-start.1 = ((bf16[64,256,128]{2,1,0:T(8,128)(2,1)}), bf16[64,256,128]{2,1,0:T(8,128)(2,1)}, u32[]{:S(2)}, u32[]{:S(2)}) async-start(bf16[64,256,128]{2,1,0:T(8,128)(2,1)} %bitcast.45), calls=%async_computation.1 | async-start | bytes 8388608 | tf_op jit(solution)/shard_map/all_to_all | solution.py:64
  91.6 19.2 %copy-start.3 = (bf16[2,256,2048]{2,1,0:T(8,128)(2,1)S(1)}, bf16[2,256,2048]{2,1,0:T(8,128)(2,1)}, u32[]{:S(2)}) copy-start(bf16[2,256,2048]{2,1,0:T(8,128)(2,1)} %param.6) | copy-start | bytes 6291460
  91.6 97.4 %all-to-all-start = ((bf16[64,256,128]{2,1,0:T(8,128)(2,1)}), bf16[64,256,128]{2,1,0:T(8,128)(2,1)}, u32[]{:S(2)}, u32[]{:S(2)}) async-start(bf16[64,256,128]{2,1,0:T(8,128)(2,1)} %bitcast.43), calls=%async_computation | async-start | bytes 8388608 | tf_op jit(solution)/shard_map/all_to_all | solution.py:63
  111.5 1.0 copy-start.17
  192.0 97.5 %all-to-all-start.2 = ((bf16[64,256,128]{2,1,0:T(8,128)(2,1)}), bf16[64,256,128]{2,1,0:T(8,128)(2,1)}, u32[]{:S(2)}, u32[]{:S(2)}) async-start(bf16[64,256,128]{2,1,0:T(8,128)(2,1)} %bitcast.44), calls=%async_computation.2 | async-start | bytes 8388608 | tf_op jit(solution)/shard_map/all_to_all | solution.py:65
  289.5 3.4 copy-start.1
  289.5 6.2 %copy-start.2 = (bf16[4,16,256,128]{3,2,1,0:T(8,128)(2,1)S(1)}, bf16[4,16,256,128]{3,2,1,0:T(8,128)(2,1)}, u32[]{:S(2)}) copy-start(bf16[4,16,256,128]{3,2,1,0:T(8,128)(2,1)} %copy.52) | copy-start | bytes 12582916
  292.3 137.4 %copy-start = (bf16[4,16,256,128]{3,2,1,0:T(8,128)(2,1)}, bf16[4,16,256,128]{3,2,1,0:T(8,128)(2,1)S(1)}, u32[]{:S(2)}) copy-start(bf16[4,16,256,128]{3,2,1,0:T(8,128)(2,1)S(1)} %copy.56) | copy-start | bytes 12582916
  295.7 4.1 copy-start.11
  304.7 7.9 %copy-start.9 = (pred[512,2048]{1,0:T(8,128)(4,1)S(1)}, pred[512,2048]{1,0:T(8,128)(4,1)}, u32[]{:S(2)}) copy-start(pred[512,2048]{1,0:T(8,128)(4,1)} %iota_compare_fusion.4) | copy-start | bytes 3145732
  312.6 9.5 %copy-start.7 = (pred[512,2560]{1,0:T(8,128)(4,1)S(1)}, pred[512,2560]{1,0:T(8,128)(4,1)}, u32[]{:S(2)}) copy-start(pred[512,2560]{1,0:T(8,128)(4,1)} %iota_compare_fusion.3) | copy-start | bytes 3932164
  322.1 10.7 %copy-start.5 = (pred[512,3072]{1,0:T(8,128)(4,1)S(1)}, pred[512,3072]{1,0:T(8,128)(4,1)}, u32[]{:S(2)}) copy-start(pred[512,3072]{1,0:T(8,128)(4,1)} %iota_compare_fusion.2) | copy-start | bytes 4718596
  332.8 12.2 %copy-start.4 = (pred[512,3584]{1,0:T(8,128)(4,1)S(1)}, pred[512,3584]{1,0:T(8,128)(4,1)}, u32[]{:S(2)}) copy-start(pred[512,3584]{1,0:T(8,128)(4,1)} %iota_compare_fusion.1) | copy-start | bytes 5505028
  379.9 4.7 copy-start.12
  379.9 10.8 %slice-start = ((s8[12582912]{0:T(1024)(128)(4,1)}), s8[4194304]{0:T(1024)(128)(4,1)S(1)}, s32[]{:S(2)}) async-start(s8[12582912]{0:T(1024)(128)(4,1)} %bitcast.78), calls=%async_computation.4 | async-start | bytes 8388608
  379.9 10.8 %slice-start.1 = ((s8[12582912]{0:T(1024)(128)(4,1)}), s8[4194304]{0:T(1024)(128)(4,1)S(1)}, s32[]{:S(2)}) async-start(s8[12582912]{0:T(1024)(128)(4,1)} %bitcast.78), calls=%async_computation.5 | async-start | bytes 8388608
  384.6 6.1 %slice-start.2 = ((s8[12582912]{0:T(1024)(128)(4,1)}), s8[4194304]{0:T(1024)(128)(4,1)S(1)}, s32[]{:S(2)}) async-start(s8[12582912]{0:T(1024)(128)(4,1)} %bitcast.78), calls=%async_computation.6 | async-start | bytes 8388608
  390.7 4.4 copy-start.10
  395.2 9.5 %copy-start.8 = (pred[512,2560]{1,0:T(8,128)(4,1)S(1)}, pred[512,2560]{1,0:T(8,128)(4,1)}, u32[]{:S(2)}) copy-start(pred[512,2560]{1,0:T(8,128)(4,1)} %iota_compare_fusion.3) | copy-start | bytes 3932164
  395.2 9.5 %copy-start.16 = (pred[4,512]{1,0:T(4,128)(4,1)S(1)}, pred[4,512]{1,0:T(4,128)(4,1)}, u32[]{:S(2)}) copy-start(pred[4,512]{1,0:T(4,128)(4,1)} %get-tuple-element.9) | copy-start | bytes 6148
  404.7 11.4 %copy-start.6 = (pred[512,3072]{1,0:T(8,128)(4,1)S(1)}, pred[512,3072]{1,0:T(8,128)(4,1)}, u32[]{:S(2)}) copy-start(pred[512,3072]{1,0:T(8,128)(4,1)} %iota_compare_fusion.2) | copy-start | bytes 4718596
  404.7 11.4 %copy-start.15 = (pred[4,512]{1,0:T(4,128)(4,1)S(1)}, pred[4,512]{1,0:T(4,128)(4,1)}, u32[]{:S(2)}) copy-start(pred[4,512]{1,0:T(4,128)(4,1)} %get-tuple-element.10) | copy-start | bytes 6148
  416.1 13.6 %copy-start.14 = (pred[4,512]{1,0:T(4,128)(4,1)S(1)}, pred[4,512]{1,0:T(4,128)(4,1)}, u32[]{:S(2)}) copy-start(pred[4,512]{1,0:T(4,128)(4,1)} %get-tuple-element.11) | copy-start | bytes 6148
  429.7 15.2 %copy-start.13 = (pred[4,512]{1,0:T(4,128)(4,1)S(1)}, pred[4,512]{1,0:T(4,128)(4,1)}, u32[]{:S(2)}) copy-start(pred[4,512]{1,0:T(4,128)(4,1)} %get-tuple-element.5) | copy-start | bytes 6148
where the time goes:
time: 602 us; the launch traced here: 596 us
  waiting for transfers between devices  195 us (32%)
  matrix products  167 us (28%)
  blocking collectives  112 us (19%)
  local copies, waits for them, and re-layouts  60.2 us (10%)
  starting transfers between devices  46.1 us (8%)
  other arithmetic  15.5 us (3%)
    all_to_all x1, blocking collectives, per_device(): lax.all_to_all(output, 'tp', split_axis=1, concat_axis=0, tiled=True)  112 us
    dot_general x8, matrix products, block_attend(): jnp.einsum('gqd,gkd->gqk', block_q, key_rows, preferred_element_type=jnp....  84.2 us
    dot_general x8, matrix products, block_attend(): jnp.einsum('gqk,gkd->gqd', weight.astype(jnp.bfloat16), value_rows, prefe...  83.1 us
    all_to_all x1, waiting for transfers between devices, per_device(): lax.all_to_all(heads_q, 'tp', split_axis=0, concat_axis=1, tiled=True)  74.4 us
    all_to_all x1, waiting for transfers between devices, per_device(): lax.all_to_all(copy_k, 'tp', split_axis=0, concat_axis=1, tiled=True)  65.4 us
    all_to_all x1, waiting for transfers between devices, per_device(): lax.all_to_all(copy_v, 'tp', split_axis=0, concat_axis=1, tiled=True)  55.3 us
    all_to_all x1, starting transfers between devices, per_device(): lax.all_to_all(copy_v, 'tp', split_axis=0, concat_axis=1, tiled=True)  19.5 us
    all_to_all x1, starting transfers between devices, per_device(): lax.all_to_all(heads_q, 'tp', split_axis=0, concat_axis=1, tiled=True)  19.2 us
  transfers between devices with their start and end apart: 3, of which 3 were waited for; matrix products, arithmetic and copies ran while one was open for 7% of the time, Pallas kernels for 0%

commit v1 on v0

v1 whole, which is shorter than its diff:
```python
import functools
import math

import jax
import jax.numpy as jnp
from jax import lax
from jax.experimental import pallas as pl
from jax.experimental.pallas import tpu as pltpu
from jax.sharding import PartitionSpec as P

HEADS = 32
KVH = 16
HD = 128
GROUP = HEADS // KVH

SOFT_CAP = 50.0
SCORE_SCALE = 1.0 / (math.sqrt(144.0) * SOFT_CAP)
EXP_SCALE = SOFT_CAP * math.log2(math.e)


def attend_kernel(heads, width, span, length_ref, packed_ref, out_ref, key_ext, total_ref):
    index = pl.program_id(0)
    valid = length_ref[0]
    count = packed_ref.shape[0]
    start = index * width

    @pl.when(index == 0)
    def _():
        key_ext[:, :HD] = packed_ref[:, (heads + 1) * HD :]
        key_ext[:, HD:] = jnp.ones((count, HD), jnp.bfloat16)

    @pl.when(start >= valid)
    def _():
        out_ref[...] = jnp.zeros_like(out_ref)

    @pl.when(start < valid)
    def _():
        rows = pl.ds(pl.multiple_of(start, width), width)
        block_q = jnp.concatenate(
            [packed_ref[rows, h * HD : (h + 1) * HD] for h in range(heads)], axis=0
        )
        total_ref[...] = jnp.zeros_like(total_ref)

        def step(block, masked):
            first = pl.multiple_of(block * span, span)
            keys = packed_ref[pl.ds(first, span), heads * HD : (heads + 1) * HD]
            score = lax.dot_general(
                block_q, keys, (((1,), (1,)), ((), ())), preferred_element_type=jnp.float32
            )
            weight = jnp.exp2(jnp.tanh(score * SCORE_SCALE) * EXP_SCALE)
            if masked:
                shape = (width, span)
                key_pos = first + lax.broadcasted_iota(jnp.int32, shape, 1)
                query_pos = start + lax.broadcasted_iota(jnp.int32, shape, 0)
                allowed = (key_pos <= query_pos) & (key_pos < valid)
                weight = jnp.concatenate(
                    [
                        jnp.where(allowed, weight[h * width : (h + 1) * width], 0.0)
                        for h in range(heads)
                    ],
                    axis=0,
                )
            total_ref[...] += jnp.dot(
                weight.astype(jnp.bfloat16),
                key_ext[pl.ds(first, span), :],
                preferred_element_type=jnp.float32,
            )

        full = jnp.minimum(start + 1, valid) // span
        stop = (jnp.minimum(start + width, valid) + span - 1) // span

        def plain(block, carry):
            step(block, False)
            return carry

        def edge(block, carry):
            step(block, True)
            return carry

        lax.fori_loop(0, full, plain, 0)
        lax.fori_loop(full, stop, edge, 0)
        live = start + lax.broadcasted_iota(jnp.int32, (width, HD), 0) < valid
        for h in range(heads):
            part = slice(h * width, (h + 1) * width)
            mixed = total_ref[part, :HD] / total_ref[part, HD:]
            out_ref[:, h * HD : (h + 1) * HD] = jnp.where(live, mixed, 0.0).astype(jnp.bfloat16)


def attend(packed, valid, heads):
    count = packed.shape[0]
    width = min(256, count)
    span = min(512, count)
    return pl.pallas_call(
        functools.partial(attend_kernel, heads, width, span),
        grid_spec=pltpu.PrefetchScalarGridSpec(
            num_scalar_prefetch=1,
            grid=(count // width,),
            in_specs=[pl.BlockSpec((count, (heads + 2) * HD), lambda i, _: (0, 0))],
            out_specs=pl.BlockSpec((width, heads * HD), lambda i, _: (i, 0)),
            scratch_shapes=[
                pltpu.VMEM((count, 2 * HD), jnp.bfloat16),
                pltpu.VMEM((heads * width, 2 * HD), jnp.float32),
            ],
        ),
        out_shape=jax.ShapeDtypeStruct((count, heads * HD), jnp.bfloat16),
        cost_estimate=pl.CostEstimate(
            flops=4 * heads * count * count * HD,
            bytes_accessed=2 * count * HD * (2 * heads + 2),
            transcendentals=heads * count * count,
        ),
        compiler_params=pltpu.CompilerParams(
            dimension_semantics=("arbitrary",), vmem_limit_bytes=40 * 1024 * 1024
        ),
    )(valid, packed)


def pack_kernel(query_ref, key_ref, value_ref, out_ref):
    out_ref[0, :, : GROUP * HD] = query_ref[0]
    out_ref[0, :, GROUP * HD : (GROUP + 1) * HD] = key_ref[0]
    out_ref[0, :, (GROUP + 1) * HD :] = value_ref[0]


def pack(queries, keys, values, s):
    rows = queries.shape[1]
    size = (GROUP + 2) * HD
    return pl.pallas_call(
        pack_kernel,
        grid=(KVH,),
        in_specs=[
            pl.BlockSpec((1, rows, GROUP * HD), lambda h: (s, 0, h)),
            pl.BlockSpec((1, rows, HD), lambda h: (s, 0, h)),
            pl.BlockSpec((1, rows, HD), lambda h: (s, 0, h)),
        ],
        out_specs=pl.BlockSpec((1, rows, size), lambda h: (h, 0, 0)),
        out_shape=jax.ShapeDtypeStruct((KVH, rows, size), jnp.bfloat16),
        cost_estimate=pl.CostEstimate(
            flops=0, bytes_accessed=4 * KVH * rows * size, transcendentals=0
        ),
    )(queries, keys, values)


def unpack_kernel(*refs):
    out_ref = refs[-1]
    for s, ref in enumerate(refs[:-1]):
        out_ref[s] = ref[0]


def unpack(returned):
    _, rows, size = returned[0].shape
    seqs = len(returned)
    return pl.pallas_call(
        unpack_kernel,
        grid=(KVH,),
        in_specs=[pl.BlockSpec((1, rows, size), lambda h: (h, 0, 0))] * seqs,
        out_specs=pl.BlockSpec((seqs, rows, size), lambda h: (0, 0, h)),
        out_shape=jax.ShapeDtypeStruct((seqs, rows, KVH * size), jnp.bfloat16),
        cost_estimate=pl.CostEstimate(
            flops=0, bytes_accessed=4 * KVH * seqs * rows * size, transcendentals=0
        ),
    )(*returned)


def exchange(array):
    return lax.all_to_all(array, "tp", split_axis=0, concat_axis=0, tiled=True)


def per_device(queries, keys, values, lengths):
    seqs, rows, _ = queries.shape
    devices = lax.axis_size("tp")
    count = devices * rows
    if KVH % devices == 0:
        owned = KVH // devices
        gathered = []
        for s in range(seqs):
            packed = pack(queries, keys, values, s).reshape(devices, owned * rows, -1)
            gathered.append(exchange(packed).reshape(devices, owned, rows, -1))
        returned = []
        for s in range(seqs):
            outs = [
                attend(gathered[s][:, o].reshape(count, -1), lengths[s : s + 1], GROUP)
                for o in range(owned)
            ]
            output = outs[0] if owned == 1 else jnp.stack(outs).reshape(owned, devices, rows, -1)
            if owned > 1:
                output = output.transpose(1, 0, 2, 3)
            back = exchange(output.reshape(devices, owned * rows, GROUP * HD))
            returned.append(back.reshape(KVH, rows, GROUP * HD))
        return unpack(returned)

    pairs = seqs * HEADS
    owned = pairs // devices
    heads_q = queries.reshape(seqs, rows, HEADS, HD)
    heads_k = jnp.repeat(keys.reshape(seqs, rows, KVH, HD), GROUP, axis=2)
    heads_v = jnp.repeat(values.reshape(seqs, rows, KVH, HD), GROUP, axis=2)
    packed = jnp.concatenate([heads_q, heads_k, heads_v], axis=3)
    packed = packed.transpose(0, 2, 1, 3).reshape(devices, owned * rows, 3 * HD)
    gathered = exchange(packed).reshape(devices, owned, rows, 3 * HD)
    outs = []
    for o in range(owned):
        seq = (lax.axis_index("tp") * owned + o) // HEADS
        valid = jnp.sum(jnp.where(jnp.arange(seqs) == seq, lengths, 0))[None]
        outs.append(attend(gathered[:, o].reshape(count, 3 * HD), valid, 1))
    output = jnp.stack(outs).reshape(owned, devices, rows, HD).transpose(1, 0, 2, 3)
    returned = exchange(output.reshape(devices, owned * rows, HD))
    return (
        returned.reshape(seqs, HEADS, rows, HD)
        .transpose(0, 2, 1, 3)
        .reshape(seqs, rows, HEADS * HD)
    )


def solution(mesh):
    placed = (
        P("groups", "tp", None),
        P("groups", "tp", None),
        P("groups", "tp", None),
        P("groups"),
    )
    return jax.shard_map(
        per_device, mesh=mesh, in_specs=placed, out_specs=P("groups", "tp", None), check_vma=False
    )
```

time: 602 us -> 323 us (0.54)
  matrix products: 167 us -> 0 us
  Pallas kernels: 0 us -> 82 us
  local copies, waits for them, and re-layouts: 60.2 us -> 0.6 us
  waiting for transfers between devices: 195 us -> 136 us
  blocking collectives: 112 us -> 58.3 us
  other arithmetic: 15.5 us -> 0 us
    dot_general x16 -> x0, matrix products: 167 us -> none  [the longest x8 84.2 us: block_attend(): jnp.einsum('gqd,gkd->gqk', block_q, key_rows, preferred_element_type=jnp....]
    pallas_call x0 -> x5, Pallas kernels: none -> 82 us  [the longest x2 51.3 us: attend(): pl.pallas_call(functools.partial(attend_kernel, heads, width, span), grid...]
    all_to_all x3, waiting for transfers between devices: 195 us -> 136 us  [exchange(): return lax.all_to_all(array, 'tp', split_axis=0, concat_axis=0, tiled=True)]
    all_to_all x1, blocking collectives: 112 us -> 58.3 us  [exchange(): return lax.all_to_all(array, 'tp', split_axis=0, concat_axis=0, tiled=True)]
    all_to_all x5 -> x0, local copies, waits for them, and re-layouts: 15 us -> none  [the longest x1 4.7 us: per_device(): lax.all_to_all(copy_k, 'tp', split_axis=0, concat_axis=1, tiled=True)]
    transpose x6 -> x0, local copies, waits for them, and re-layouts: 14.5 us -> none  [the longest x1 6.33 us: per_device(): queries.reshape(seqs, rows, HEADS, HD).transpose(0, 2, 1, 3)]
    le x8 -> x0, other arithmetic: 14.1 us -> none  [block_attend(): key_pos[None, None, :] <= query_pos[None, :, None]]
    unnamed x45 -> x2, local copies, waits for them, and re-layouts: 12.7 us -> 0.01 us
  transfers between devices with their start and end apart: 3 -> 3, of which waited for: 3 -> 3; matrix products, arithmetic and copies ran while one was open for 7% -> 0% of each run, Pallas kernels for 0% -> 19%
where the time goes in v1:
time: 323 us; the launch traced here: 322 us
  waiting for transfers between devices  136 us (42%)
  Pallas kernels  82 us (25%)
  blocking collectives  58.3 us (18%)
  starting transfers between devices  45.5 us (14%)
    all_to_all x3, waiting for transfers between devices, exchange(): return lax.all_to_all(array, 'tp', split_axis=0, concat_axis=0, tiled=True)  136 us
    all_to_all x1, blocking collectives, exchange(): return lax.all_to_all(array, 'tp', split_axis=0, concat_axis=0, tiled=True)  58.3 us
    pallas_call x2, Pallas kernels, attend(): pl.pallas_call(functools.partial(attend_kernel, heads, width, span), grid...  51.3 us
    all_to_all x3, starting transfers between devices, exchange(): return lax.all_to_all(array, 'tp', split_axis=0, concat_axis=0, tiled=True)  45.5 us
    pallas_call x2, Pallas kernels, pack(): pl.pallas_call(pack_kernel, grid=(KVH,), in_specs=[pl.BlockSpec((1, rows,...  20.4 us
    pallas_call x1, Pallas kernels, unpack(): pl.pallas_call(unpack_kernel, grid=(KVH,), in_specs=[pl.BlockSpec((1, row...  10.3 us
  transfers between devices with their start and end apart: 3, of which 3 were waited for; matrix products, arithmetic and copies ran while one was open for 0% of the time, Pallas kernels for 19%

profile of v1, /device:TPU:1, one launch (start us, length us, event | category | flops | bytes accessed | tf_op | source)
XLA Modules:
  0.0 322.2 jit_solution(1650353399023940170)
XLA Ops:
  0.0 10.2 %shard_map.48 = bf16[16,256,512]{2,1,0:T(8,128)(2,1)} custom-call(bf16[2,256,4096]{2,1,0:T(8,128)(2,1)} %query_ref.3, bf16[2,256,2048]{2,1,0:T(8,128)(2,1)} %key_ref.3, bf16[2,256,2048]{2,1,0:T(8,128)(2,1)} %value_ref.3), custom_call_target="tpu_custom_call" | custom-call | bytes 8388608 | tf_op jit(solution)/shard_map/pallas_call | solution.py:126
  10.2 7.3 %all-to-all-start.2 = ((bf16[16,256,512]{2,1,0:T(8,128)(2,1)}), bf16[16,256,512]{2,1,0:T(8,128)(2,1)}, u32[]{:S(2)}, u32[]{:S(2)}) async-start(bf16[16,256,512]{2,1,0:T(8,128)(2,1)} %shard_map.48), calls=%async_computation.2 | async-start | bytes 8388608 | tf_op jit(solution)/shard_map/all_to_all | solution.py:164
  17.5 10.2 %shard_map.46 = bf16[16,256,512]{2,1,0:T(8,128)(2,1)} custom-call(bf16[2,256,4096]{2,1,0:T(8,128)(2,1)} %query_ref.3, bf16[2,256,2048]{2,1,0:T(8,128)(2,1)} %key_ref.3, bf16[2,256,2048]{2,1,0:T(8,128)(2,1)} %value_ref.3), custom_call_target="tpu_custom_call" | custom-call | bytes 8388608 | tf_op jit(solution)/shard_map/pallas_call | solution.py:126
  27.7 0.0 copy-start
  27.7 67.9 %all-to-all-done.2 = bf16[16,256,512]{2,1,0:T(8,128)(2,1)} async-done(((bf16[16,256,512]{2,1,0:T(8,128)(2,1)}), bf16[16,256,512]{2,1,0:T(8,128)(2,1)}, u32[]{:S(2)}, u32[]{:S(2)}) %all-to-all-start.2) | async-done | bytes 4194336 | tf_op jit(solution)/shard_map/all_to_all | solution.py:164
  95.7 19.1 %all-to-all-start = ((bf16[16,256,512]{2,1,0:T(8,128)(2,1)}), bf16[16,256,512]{2,1,0:T(8,128)(2,1)}, u32[]{:S(2)}, u32[]{:S(2)}) async-start(bf16[16,256,512]{2,1,0:T(8,128)(2,1)} %shard_map.46), calls=%async_computation | async-start | bytes 8388608 | tf_op jit(solution)/shard_map/all_to_all | solution.py:164
  114.8 0.0 copy-done
  114.8 0.6 fusion
  115.4 30.0 %shard_map.49 = bf16[4096,256]{1,0:T(8,128)(2,1)} custom-call(s32[1]{0:T(128)} %get-tuple-element.5.length_ref, bf16[4096,512]{1,0:T(8,128)(2,1)} %bitcast.2.packed_ref), custom_call_target="tpu_custom_call" | custom-call | flops 17179869184 | bytes 6291456 | tf_op jit(solution)/shard_map/pallas_call | solution.py:93
  145.4 47.5 %all-to-all-done = bf16[16,256,512]{2,1,0:T(8,128)(2,1)} async-done(((bf16[16,256,512]{2,1,0:T(8,128)(2,1)}), bf16[16,256,512]{2,1,0:T(8,128)(2,1)}, u32[]{:S(2)}, u32[]{:S(2)}) %all-to-all-start) | async-done | bytes 4194336 | tf_op jit(solution)/shard_map/all_to_all | solution.py:164
  192.9 19.1 %all-to-all-start.3 = ((bf16[16,256,256]{2,1,0:T(8,128)(2,1)}), bf16[16,256,256]{2,1,0:T(8,128)(2,1)}, u32[]{:S(2)}, u32[]{:S(2)}) async-start(bf16[16,256,256]{2,1,0:T(8,128)(2,1)} %bitcast.3), calls=%async_computation.3 | async-start | bytes 4194304 | tf_op jit(solution)/shard_map/all_to_all | solution.py:164
  212.0 21.3 %shard_map.47 = bf16[4096,256]{1,0:T(8,128)(2,1)S(1)} custom-call(s32[1]{0:T(128)} %get-tuple-element.6.length_ref, bf16[4096,512]{1,0:T(8,128)(2,1)} %bitcast.packed_ref), custom_call_target="tpu_custom_call" | custom-call | flops 17179869184 | bytes 6291456 | tf_op jit(solution)/shard_map/pallas_call | solution.py:93
  233.3 20.3 %all-to-all-done.3.refs_1_ = bf16[16,256,256]{2,1,0:T(8,128)(2,1)} async-done(((bf16[16,256,256]{2,1,0:T(8,128)(2,1)}), bf16[16,256,256]{2,1,0:T(8,128)(2,1)}, u32[]{:S(2)}, u32[]{:S(2)}) %all-to-all-start.3) | async-done | bytes 2097184 | tf_op jit(solution)/shard_map/all_to_all | solution.py:164
  253.6 58.3 %all_to_all.20.refs_0_ = bf16[16,256,256]{2,1,0:T(8,128)(2,1)} all-to-all(bf16[16,256,256]{2,1,0:T(8,128)(2,1)S(1)} %bitcast.4), channel_id=1, replica_groups=mesh['groups'=2,'tp'=16] {'tp'}, dimensions={0} | all-to-all | bytes 4194304 | tf_op jit(solution)/shard_map/all_to_all | solution.py:164
  311.9 10.3 %shard_map.50 = bf16[2,256,4096]{2,1,0:T(8,128)(2,1)} custom-call(bf16[16,256,256]{2,1,0:T(8,128)(2,1)} %all_to_all.20.refs_0_, bf16[16,256,256]{2,1,0:T(8,128)(2,1)} %all-to-all-done.3.refs_1_), custom_call_target="tpu_custom_call" | custom-call | bytes 8388608 | tf_op jit(solution)/shard_map/pallas_call | solution.py:151
Async XLA Ops:
  10.2 85.5 %all-to-all-start.2 = ((bf16[16,256,512]{2,1,0:T(8,128)(2,1)}), bf16[16,256,512]{2,1,0:T(8,128)(2,1)}, u32[]{:S(2)}, u32[]{:S(2)}) async-start(bf16[16,256,512]{2,1,0:T(8,128)(2,1)} %shard_map.48), calls=%async_computation.2 | async-start | bytes 8388608 | tf_op jit(solution)/shard_map/all_to_all | solution.py:164
  27.7 87.0 %copy-start = (s32[2]{0:T(128)S(1)}, s32[2]{0:T(128)}, u32[]{:S(2)}) copy-start(s32[2]{0:T(128)} %param.7) | copy-start | bytes 28
  95.7 97.2 %all-to-all-start = ((bf16[16,256,512]{2,1,0:T(8,128)(2,1)}), bf16[16,256,512]{2,1,0:T(8,128)(2,1)}, u32[]{:S(2)}, u32[]{:S(2)}) async-start(bf16[16,256,512]{2,1,0:T(8,128)(2,1)} %shard_map.46), calls=%async_computation | async-start | bytes 8388608 | tf_op jit(solution)/shard_map/all_to_all | solution.py:164
  192.9 60.7 %all-to-all-start.3 = ((bf16[16,256,256]{2,1,0:T(8,128)(2,1)}), bf16[16,256,256]{2,1,0:T(8,128)(2,1)}, u32[]{:S(2)}, u32[]{:S(2)}) async-start(bf16[16,256,256]{2,1,0:T(8,128)(2,1)} %bitcast.3), calls=%async_computation.3 | async-start | bytes 4194304 | tf_op jit(solution)/shard_map/all_to_all | solution.py:164

commit v2 on v1

v2 whole, which is shorter than its diff:
```python
import functools
import math

import jax
import jax.numpy as jnp
from jax import lax
from jax.experimental import pallas as pl
from jax.experimental.pallas import tpu as pltpu
from jax.sharding import PartitionSpec as P


HEADS = 32
KVH = 16
HD = 128
GROUP = HEADS // KVH

SOFT_CAP = 50.0
SCORE_SCALE = 1.0 / (math.sqrt(144.0) * SOFT_CAP)
EXP_SCALE = SOFT_CAP * math.log2(math.e)


def attend_half_kernel(
    width, span, info_ref, query_ref, own_ref, early_ref, out_ref, key_all, value_ext, total_ref
):
    index = pl.program_id(0)
    valid = info_ref[0]
    base = pl.multiple_of(info_ref[1], span)
    blocks, _, rows, _ = own_ref.shape
    part = blocks * rows
    start = base + index * width

    @pl.when((index == 0) & (base < valid))
    def _():
        early = early_ref[...].reshape(part, 2 * HD)
        key_all[:part, :] = early[:, :HD]
        value_ext[:part, :HD] = early[:, HD:]
        own = own_ref[:, 0].reshape(part, 2 * HD)
        key_all[pl.ds(base, part), :] = own[:, :HD]
        value_ext[pl.ds(base, part), :HD] = own[:, HD:]
        value_ext[:, HD:] = jnp.ones((2 * part, HD), jnp.bfloat16)

    attend_block(
        GROUP, width, span, start, valid, query_ref, (0, 0), key_all, value_ext, out_ref, (0,), total_ref
    )


def attend_block(
    heads, width, span, start, valid, query_ref, at_q, key_all, value_ext, out_ref, at_o, total_ref
):
    @pl.when(start >= valid)
    def _():
        out_ref[...] = jnp.zeros_like(out_ref)

    @pl.when(start < valid)
    def _():
        block_q = jnp.concatenate(
            [query_ref[at_q + (slice(None), slice(h * HD, (h + 1) * HD))] for h in range(heads)],
            axis=0,
        )
        total_ref[...] = jnp.zeros_like(total_ref)

        def step(block, masked):
            first = pl.multiple_of(block * span, span)
            score = lax.dot_general(
                block_q,
                key_all[pl.ds(first, span), :],
                (((1,), (1,)), ((), ())),
                preferred_element_type=jnp.float32,
            )
            weight = jnp.exp2(jnp.tanh(score * SCORE_SCALE) * EXP_SCALE)
            if masked:
                shape = (width, span)
                key_pos = first + lax.broadcasted_iota(jnp.int32, shape, 1)
                query_pos = start + lax.broadcasted_iota(jnp.int32, shape, 0)
                allowed = (key_pos <= query_pos) & (key_pos < valid)
                weight = jnp.concatenate(
                    [
                        jnp.where(allowed, weight[h * width : (h + 1) * width], 0.0)
                        for h in range(heads)
                    ],
                    axis=0,
                )
            total_ref[...] += jnp.dot(
                weight.astype(jnp.bfloat16),
                value_ext[pl.ds(first, span), :],
                preferred_element_type=jnp.float32,
            )

        full = jnp.minimum(start + 1, valid) // span
        stop = (jnp.minimum(start + width, valid) + span - 1) // span

        def plain(block, carry):
            step(block, False)
            return carry

        def edge(block, carry):
            step(block, True)
            return carry

        lax.fori_loop(0, full, plain, 0)
        lax.fori_loop(full, stop, edge, 0)
        live = start + lax.broadcasted_iota(jnp.int32, (width, HD), 0) < valid
        for h in range(heads):
            part = slice(h * width, (h + 1) * width)
            mixed = total_ref[part, :HD] / total_ref[part, HD:]
            out_ref[at_o + (slice(None), slice(h * HD, (h + 1) * HD))] = jnp.where(
                live, mixed, 0.0
            ).astype(jnp.bfloat16)


def attend_half(query, own, early, info, which):
    half, _, rows, size = query.shape
    part = half * rows
    span = min(512, part)
    return pl.pallas_call(
        functools.partial(attend_half_kernel, rows, span),
        grid_spec=pltpu.PrefetchScalarGridSpec(
            num_scalar_prefetch=1,
            grid=(half,),
            in_specs=[
                pl.BlockSpec((1, 1, rows, size), lambda i, _: (i, which, 0, 0)),
                pl.BlockSpec((half, 1, rows, 2 * HD), lambda i, _: (0, which, 0, 0)),
                pl.BlockSpec((half, rows, 2 * HD), lambda i, _: (0, 0, 0)),
            ],
            out_specs=pl.BlockSpec((1, rows, size), lambda i, _: (i, 0, 0)),
            scratch_shapes=[
                pltpu.VMEM((2 * part, HD), jnp.bfloat16),
                pltpu.VMEM((2 * part, 2 * HD), jnp.bfloat16),
                pltpu.VMEM((GROUP * rows, 2 * HD), jnp.float32),
            ],
        ),
        out_shape=jax.ShapeDtypeStruct((half, rows, size), jnp.bfloat16),
        cost_estimate=pl.CostEstimate(
            flops=6 * GROUP * part * part * HD,
            bytes_accessed=2 * part * HD * 8,
            transcendentals=GROUP * part * part,
        ),
        compiler_params=pltpu.CompilerParams(
            dimension_semantics=("arbitrary",), vmem_limit_bytes=40 * 1024 * 1024
        ),
    )(info, query, own, early)


def attend_kernel(heads, width, span, length_ref, packed_ref, out_ref, key_all, value_ext, total_ref):
    index = pl.program_id(0)
    count = packed_ref.shape[0]
    start = pl.multiple_of(index * width, width)

    @pl.when(index == 0)
    def _():
        key_all[...] = packed_ref[:, heads * HD : (heads + 1) * HD]
        value_ext[:, :HD] = packed_ref[:, (heads + 1) * HD :]
        value_ext[:, HD:] = jnp.ones((count, HD), jnp.bfloat16)

    query = packed_ref.at[pl.ds(start, width)]
    attend_block(
        heads, width, span, start, length_ref[0], query, (), key_all, value_ext, out_ref, (), total_ref
    )


def attend(packed, valid, heads):
    count = packed.shape[0]
    width = min(256, count)
    span = min(512, count)
    return pl.pallas_call(
        functools.partial(attend_kernel, heads, width, span),
        grid_spec=pltpu.PrefetchScalarGridSpec(
            num_scalar_prefetch=1,
            grid=(count // width,),
            in_specs=[pl.BlockSpec((count, (heads + 2) * HD), lambda i, _: (0, 0))],
            out_specs=pl.BlockSpec((width, heads * HD), lambda i, _: (i, 0)),
            scratch_shapes=[
                pltpu.VMEM((count, HD), jnp.bfloat16),
                pltpu.VMEM((count, 2 * HD), jnp.bfloat16),
                pltpu.VMEM((heads * width, 2 * HD), jnp.float32),
            ],
        ),
        out_shape=jax.ShapeDtypeStruct((count, heads * HD), jnp.bfloat16),
        cost_estimate=pl.CostEstimate(
            flops=4 * heads * count * count * HD,
            bytes_accessed=2 * count * HD * (2 * heads + 2),
            transcendentals=heads * count * count,
        ),
        compiler_params=pltpu.CompilerParams(
            dimension_semantics=("arbitrary",), vmem_limit_bytes=40 * 1024 * 1024
        ),
    )(valid, packed)


def pack_kernel(take, *refs):
    out_ref = refs[-1]
    for h in range(take):
        first = 0
        for ref in refs[:-1]:
            size = ref.shape[2] // take
            out_ref[h, :, first : first + size] = ref[0, :, h * size : (h + 1) * size]
            first += size


def pack(arrays, s):
    rows = arrays[0].shape[1]
    take = min(4, KVH)
    sizes = [a.shape[2] // KVH for a in arrays]
    total = sum(sizes)
    return pl.pallas_call(
        functools.partial(pack_kernel, take),
        grid=(KVH // take,),
        in_specs=[pl.BlockSpec((1, rows, take * size), lambda h: (s, 0, h)) for size in sizes],
        out_specs=pl.BlockSpec((take, rows, total), lambda h: (h, 0, 0)),
        out_shape=jax.ShapeDtypeStruct((KVH, rows, total), jnp.bfloat16),
        cost_estimate=pl.CostEstimate(
            flops=0, bytes_accessed=4 * KVH * rows * total, transcendentals=0
        ),
    )(*arrays)


def unpack_kernel(take, owned, *refs):
    out_ref = refs[-1]
    size = refs[0].shape[2]
    for d in range(take):
        for n, ref in enumerate(refs[:-1]):
            s, o = n // owned, n % owned
            first = (d * owned + o) * size
            out_ref[s, :, first : first + size] = ref[d]


def unpack(returned, owned):
    half, rows, size = returned[0].shape
    seqs = len(returned) // owned
    take = min(2, half)
    return pl.pallas_call(
        functools.partial(unpack_kernel, take, owned),
        grid=(half // take,),
        in_specs=[pl.BlockSpec((take, rows, size), lambda d: (d, 0, 0))] * len(returned),
        out_specs=pl.BlockSpec((seqs, rows, take * owned * size), lambda d: (0, 0, d)),
        out_shape=jax.ShapeDtypeStruct((seqs, rows, half * owned * size), jnp.bfloat16),
        cost_estimate=pl.CostEstimate(
            flops=0, bytes_accessed=4 * half * owned * seqs * rows * size, transcendentals=0
        ),
    )(*returned)


def exchange(array, groups=None):
    return lax.all_to_all(
        array, "tp", split_axis=0, concat_axis=0, tiled=True, axis_index_groups=groups
    )


def by_halves(queries, keys, values, lengths):
    seqs, rows, _ = queries.shape
    devices = lax.axis_size("tp")
    half = devices // 2
    owned = KVH // half
    groups = [list(range(half)), list(range(half, devices))]
    forward = [(j, half + j) for j in range(half)]
    base = jnp.where(lax.axis_index("tp") >= half, half * rows, 0).astype(jnp.int32)
    held = []
    for s in range(seqs):
        packed = pack((keys, values), s).reshape(half, owned * rows, -1)
        pair = exchange(packed, groups)
        pair = pair.reshape(half, owned, rows, -1)
        early = []
        for o in range(owned):
            part = pair[:, o]
            early.append(lax.ppermute(part, "tp", forward))
        packed = pack((queries,), s).reshape(half, owned * rows, -1)
        query = exchange(packed, groups)
        held.append((query.reshape(half, owned, rows, -1), pair, early))
    returned = []
    for s in range(seqs):
        query, pair, early = held[s]
        info = jnp.stack([lengths[s], base])
        for o in range(owned):
            returned.append(exchange(attend_half(query, pair, early[o], info, o), groups))
    return unpack(returned, owned)


def halves_fit(devices):
    return devices % 2 == 0 and KVH % (devices // 2) == 0


def per_device(queries, keys, values, lengths):
    seqs, rows, _ = queries.shape
    devices = lax.axis_size("tp")
    count = devices * rows
    if halves_fit(devices):
        return by_halves(queries, keys, values, lengths)

    pairs = seqs * HEADS
    owned = pairs // devices
    heads_q = queries.reshape(seqs, rows, HEADS, HD)
    heads_k = jnp.repeat(keys.reshape(seqs, rows, KVH, HD), GROUP, axis=2)
    heads_v = jnp.repeat(values.reshape(seqs, rows, KVH, HD), GROUP, axis=2)
    packed = jnp.concatenate([heads_q, heads_k, heads_v], axis=3)
    packed = packed.transpose(0, 2, 1, 3).reshape(devices, owned * rows, 3 * HD)
    gathered = exchange(packed).reshape(devices, owned, rows, 3 * HD)
    outs = []
    for o in range(owned):
        seq = (lax.axis_index("tp") * owned + o) // HEADS
        valid = jnp.sum(jnp.where(jnp.arange(seqs) == seq, lengths, 0))[None]
        outs.append(attend(gathered[:, o].reshape(count, 3 * HD), valid, 1))
    output = jnp.stack(outs).reshape(owned, devices, rows, HD).transpose(1, 0, 2, 3)
    returned = exchange(output.reshape(devices, owned * rows, HD))
    return (
        returned.reshape(seqs, HEADS, rows, HD)
        .transpose(0, 2, 1, 3)
        .reshape(seqs, rows, HEADS * HD)
    )


def solution(mesh):
    placed = (
        P("groups", "tp", None),
        P("groups", "tp", None),
        P("groups", "tp", None),
        P("groups"),
    )
    return jax.shard_map(
        per_device, mesh=mesh, in_specs=placed, out_specs=P("groups", "tp", None), check_vma=False
    )
```

time: 323 us -> 426 us (1.32)
  the two profiles are of different devices: /device:TPU:1 before, /device:TPU:18 now
where the time goes in v2:
time: 426 us; the launch traced here: 424 us
  waiting for transfers between devices  214 us (50%)
  Pallas kernels  89.1 us (21%)
  starting transfers between devices  65.1 us (15%)
  blocking collectives  40.7 us (10%)
  local copies, waits for them, and re-layouts  13.9 us (3%)
    ppermute x4, waiting for transfers between devices, by_halves(): early.append(lax.ppermute(part, 'tp', forward))  149 us
    pallas_call x4, Pallas kernels, attend_half(): pl.pallas_call(functools.partial(attend_half_kernel, rows, span), grid_sp...  68.9 us
    all_to_all x7, waiting for transfers between devices, exchange(): lax.all_to_all(array, 'tp', split_axis=0, concat_axis=0, tiled=True, axis...  65.4 us
    all_to_all x7, starting transfers between devices, exchange(): lax.all_to_all(array, 'tp', split_axis=0, concat_axis=0, tiled=True, axis...  60 us
    all_to_all x1, blocking collectives, exchange(): lax.all_to_all(array, 'tp', split_axis=0, concat_axis=0, tiled=True, axis...  40.7 us
    pallas_call x4, Pallas kernels, pack(): pl.pallas_call(functools.partial(pack_kernel, take), grid=(KVH // take,),...  15.4 us
    unnamed x18, local copies, waits for them, and re-layouts  9 us
  transfers between devices with their start and end apart: 11, of which 7 were waited for; matrix products, arithmetic and copies ran while one was open for 1% of the time, Pallas kernels for 19%

profile of v2, /device:TPU:18, one launch (start us, length us, event | category | flops | bytes accessed | tf_op | source)
XLA Modules:
  0.0 424.2 jit_solution(4284046263333821575)
XLA Ops:
  0.0 3.8 shard_map.46
  3.8 3.8 all-to-all-start
  7.6 3.9 shard_map.47
  11.5 21.8 %all-to-all-done = bf16[8,512,256]{2,1,0:T(8,128)(2,1)S(1)} async-done(((bf16[8,512,256]{2,1,0:T(8,128)(2,1)}), bf16[8,512,256]{2,1,0:T(8,128)(2,1)S(1)}, u32[]{:S(2)}, u32[]{:S(2)}) %all-to-all-start) | async-done | bytes 2097184 | tf_op jit(solution)/shard_map/all_to_all | solution.py:244
  33.3 0.0 copy-start.3
  33.3 1.3 copy-done.3
  34.6 3.6 all-to-all-start.1
  38.2 3.9 shard_map.50
  42.1 21.8 %all-to-all-done.1 = bf16[8,512,256]{2,1,0:T(8,128)(2,1)S(1)} async-done(((bf16[8,512,256]{2,1,0:T(8,128)(2,1)}), bf16[8,512,256]{2,1,0:T(8,128)(2,1)S(1)}, u32[]{:S(2)}, u32[]{:S(2)}) %all-to-all-start.1) | async-done | bytes 2097184 | tf_op jit(solution)/shard_map/all_to_all | solution.py:244
  63.9 1.3 copy-done
  65.2 4.3 %all-to-all-start.4 = ((bf16[8,512,256]{2,1,0:T(8,128)(2,1)}), bf16[8,512,256]{2,1,0:T(8,128)(2,1)}, u32[]{:S(2)}, u32[]{:S(2)}) async-start(bf16[8,512,256]{2,1,0:T(8,128)(2,1)} %bitcast.35), calls=%async_computation.4 | async-start | bytes 4194304 | tf_op jit(solution)/shard_map/all_to_all | solution.py:244
  69.5 3.9 shard_map.51
  73.4 21.8 %all-to-all-done.4 = bf16[8,512,256]{2,1,0:T(8,128)(2,1)} async-done(((bf16[8,512,256]{2,1,0:T(8,128)(2,1)}), bf16[8,512,256]{2,1,0:T(8,128)(2,1)}, u32[]{:S(2)}, u32[]{:S(2)}) %all-to-all-start.4) | async-done | bytes 2097184 | tf_op jit(solution)/shard_map/all_to_all | solution.py:244
  95.2 3.6 all-to-all-start.5
  98.8 0.0 copy-start.8
  98.9 3.1 slice_bitcast_fusion.2
  102.0 1.3 collective-permute-start
  103.3 0.0 copy-done.8
  103.3 0.6 fusion
  103.8 0.7 pad_add_fusion.info_ref
  104.6 41.2 %collective-permute-done.early_ref = bf16[8,256,256]{2,1,0:T(8,128)(2,1)S(1)} collective-permute-done((bf16[8,256,256]{2,1,0:T(8,128)(2,1)}, bf16[8,256,256]{2,1,0:T(8,128)(2,1)S(1)}, u32[]{:S(2)}, u32[]{:S(2)}) %collective-permute-start) | collective-permute-done | bytes 1048608 | tf_op jit(solution)/shard_map/ppermute | solution.py:265
  145.7 1.6 copy-done.1
  147.3 1.6 copy-done.4
  148.9 6.7 %shard_map.48 = bf16[8,256,256]{2,1,0:T(8,128)(2,1)} custom-call(s32[2]{0:T(128)S(1)} %pad_add_fusion.info_ref, bf16[8,2,256,256]{3,2,1,0:T(8,128)(2,1)S(1)} %bitcast.31, bf16[8,2,256,256]{3,2,1,0:T(8,128)(2,1)S(1)} %bitcast.29, bf16[8,256,256]{2,1,0:T(8,128)(2,1)S(1)} %collective-permute-done.early_ref), custom_call_target="tpu_custom_call" | custom-call | flops 6442450944 | bytes 4194304 | tf_op jit(solution)/shard_map/pallas_call | solution.py:115
  155.6 0.0 all-to-all-done.5
  155.6 11.1 %all-to-all-start.2 = ((bf16[8,256,256]{2,1,0:T(8,128)(2,1)}), bf16[8,256,256]{2,1,0:T(8,128)(2,1)S(1)}, u32[]{:S(2)}, u32[]{:S(2)}) async-start(bf16[8,256,256]{2,1,0:T(8,128)(2,1)} %shard_map.48), calls=%async_computation.2 | async-start | bytes 2097152 | tf_op jit(solution)/shard_map/all_to_all | solution.py:244
  166.7 1.3 collective-permute-start.1
  168.0 41.0 %collective-permute-done.1.early_ref = bf16[8,256,256]{2,1,0:T(8,128)(2,1)S(1)} collective-permute-done((bf16[8,256,256]{2,1,0:T(8,128)(2,1)}, bf16[8,256,256]{2,1,0:T(8,128)(2,1)S(1)}, u32[]{:S(2)}, u32[]{:S(2)}) %collective-permute-start.1) | collective-permute-done | bytes 1048608 | tf_op jit(solution)/shard_map/ppermute | solution.py:265
  209.0 1.6 copy-done.2
  210.6 1.6 copy-done.5
  212.2 6.7 %shard_map.49 = bf16[8,256,256]{2,1,0:T(8,128)(2,1)} custom-call(s32[2]{0:T(128)S(1)} %pad_add_fusion.info_ref, bf16[8,2,256,256]{3,2,1,0:T(8,128)(2,1)S(1)} %bitcast.32, bf16[8,2,256,256]{3,2,1,0:T(8,128)(2,1)S(1)} %bitcast.30, bf16[8,256,256]{2,1,0:T(8,128)(2,1)S(1)} %collective-permute-done.1.early_ref), custom_call_target="tpu_custom_call" | custom-call | flops 6442450944 | bytes 4194304 | tf_op jit(solution)/shard_map/pallas_call | solution.py:115
  218.9 0.0 all-to-all-done.2.refs_0_
  218.9 16.2 %all-to-all-start.3 = ((bf16[8,256,256]{2,1,0:T(8,128)(2,1)}), bf16[8,256,256]{2,1,0:T(8,128)(2,1)}, u32[]{:S(2)}, u32[]{:S(2)}) async-start(bf16[8,256,256]{2,1,0:T(8,128)(2,1)} %shard_map.49), calls=%async_computation.3 | async-start | bytes 2097152 | tf_op jit(solution)/shard_map/all_to_all | solution.py:244
  235.1 1.2 slice_bitcast_fusion
  236.3 0.0 copy-done.6
  236.3 1.3 collective-permute-start.2
  237.6 0.6 pad_add_fusion.1.info_ref
  238.2 39.2 %collective-permute-done.2.early_ref = bf16[8,256,256]{2,1,0:T(8,128)(2,1)S(1)} collective-permute-done((bf16[8,256,256]{2,1,0:T(8,128)(2,1)S(1)}, bf16[8,256,256]{2,1,0:T(8,128)(2,1)S(1)}, u32[]{:S(2)}, u32[]{:S(2)}) %collective-permute-start.2) | collective-permute-done | bytes 1048608 | tf_op jit(solution)/shard_map/ppermute | solution.py:265
  277.4 28.1 %shard_map.52 = bf16[8,256,256]{2,1,0:T(8,128)(2,1)} custom-call(s32[2]{0:T(128)S(1)} %pad_add_fusion.1.info_ref, bf16[8,2,256,256]{3,2,1,0:T(8,128)(2,1)} %bitcast.8.query_ref, bf16[8,2,256,256]{3,2,1,0:T(8,128)(2,1)S(1)} %bitcast.26, bf16[8,256,256]{2,1,0:T(8,128)(2,1)S(1)} %collective-permute-done.2.early_ref), custom_call_target="tpu_custom_call" | custom-call | flops 6442450944 | bytes 4194304 | tf_op jit(solution)/shard_map/pallas_call | solution.py:115
  305.5 0.0 all-to-all-done.3.refs_1_
  305.5 17.3 %all-to-all-start.6 = ((bf16[8,256,256]{2,1,0:T(8,128)(2,1)}), bf16[8,256,256]{2,1,0:T(8,128)(2,1)}, u32[]{:S(2)}, u32[]{:S(2)}) async-start(bf16[8,256,256]{2,1,0:T(8,128)(2,1)} %shard_map.52), calls=%async_computation.6 | async-start | bytes 2097152 | tf_op jit(solution)/shard_map/all_to_all | solution.py:244
  322.9 0.0 copy-done.7
  322.9 1.3 collective-permute-start.3
  324.2 27.1 %collective-permute-done.3.early_ref = bf16[8,256,256]{2,1,0:T(8,128)(2,1)S(1)} collective-permute-done((bf16[8,256,256]{2,1,0:T(8,128)(2,1)S(1)}, bf16[8,256,256]{2,1,0:T(8,128)(2,1)S(1)}, u32[]{:S(2)}, u32[]{:S(2)}) %collective-permute-start.3) | collective-permute-done | bytes 1048608 | tf_op jit(solution)/shard_map/ppermute | solution.py:265
  351.3 27.4 %shard_map.53 = bf16[8,256,256]{2,1,0:T(8,128)(2,1)S(1)} custom-call(s32[2]{0:T(128)S(1)} %pad_add_fusion.1.info_ref, bf16[8,2,256,256]{3,2,1,0:T(8,128)(2,1)} %bitcast.8.query_ref, bf16[8,2,256,256]{3,2,1,0:T(8,128)(2,1)S(1)} %bitcast.27, bf16[8,256,256]{2,1,0:T(8,128)(2,1)S(1)} %collective-permute-done.3.early_ref), custom_call_target="tpu_custom_call" | custom-call | flops 6442450944 | bytes 4194304 | tf_op jit(solution)/shard_map/pallas_call | solution.py:115
  378.7 0.0 all-to-all-done.6.refs_2_
  378.7 40.7 %all_to_all.40.refs_3_ = bf16[8,256,256]{2,1,0:T(8,128)(2,1)} all-to-all(bf16[8,256,256]{2,1,0:T(8,128)(2,1)S(1)} %shard_map.53), channel_id=1, replica_groups={{0,1,2,3,4,5,6,7},{8,9,10,11,12,13,14,15},{16,17,18,19,20,21,22,23},{24..., dimensions={0} | all-to-all | bytes 2097152 | tf_op jit(solution)/shard_map/all_to_all | solution.py:244
  419.4 4.8 %shard_map.54 = bf16[2,256,4096]{2,1,0:T(8,128)(2,1)} custom-call(bf16[8,256,256]{2,1,0:T(8,128)(2,1)} %copy-done.6, bf16[8,256,256]{2,1,0:T(8,128)(2,1)} %all-to-all-done.3.refs_1_, bf16[8,256,256]{2,1,0:T(8,128)(2,1)} %all-to-all-done.6.refs_2_, bf16[8,256,256]{2,1,0:T(8,128)(2,1)} %all_to_all.40.refs_3_), custom_call_target="tpu_custom_call" | custom-call | bytes 8388608 | tf_op jit(solution)/shard_map/pallas_call | solution.py:231
  (7 shorter events, 0.0 us)
Async XLA Ops:
  3.8 29.5 %all-to-all-start = ((bf16[8,512,256]{2,1,0:T(8,128)(2,1)}), bf16[8,512,256]{2,1,0:T(8,128)(2,1)S(1)}, u32[]{:S(2)}, u32[]{:S(2)}) async-start(bf16[8,512,256]{2,1,0:T(8,128)(2,1)} %bitcast.36), calls=%async_computation | async-start | bytes 4194304 | tf_op jit(solution)/shard_map/all_to_all | solution.py:244
  33.3 1.3 copy-start.3
  34.6 29.2 %all-to-all-start.1 = ((bf16[8,512,256]{2,1,0:T(8,128)(2,1)}), bf16[8,512,256]{2,1,0:T(8,128)(2,1)S(1)}, u32[]{:S(2)}, u32[]{:S(2)}) async-start(bf16[8,512,256]{2,1,0:T(8,128)(2,1)} %bitcast.34), calls=%async_computation.1 | async-start | bytes 4194304 | tf_op jit(solution)/shard_map/all_to_all | solution.py:244
  63.9 1.3 copy-start
  65.2 30.1 %all-to-all-start.4 = ((bf16[8,512,256]{2,1,0:T(8,128)(2,1)}), bf16[8,512,256]{2,1,0:T(8,128)(2,1)}, u32[]{:S(2)}, u32[]{:S(2)}) async-start(bf16[8,512,256]{2,1,0:T(8,128)(2,1)} %bitcast.35), calls=%async_computation.4 | async-start | bytes 4194304 | tf_op jit(solution)/shard_map/all_to_all | solution.py:244
  95.2 60.4 %all-to-all-start.5 = ((bf16[8,512,256]{2,1,0:T(8,128)(2,1)}), bf16[8,512,256]{2,1,0:T(8,128)(2,1)S(1)}, u32[]{:S(2)}, u32[]{:S(2)}) async-start(bf16[8,512,256]{2,1,0:T(8,128)(2,1)} %bitcast.33), calls=%async_computation.5 | async-start | bytes 4194304 | tf_op jit(solution)/shard_map/all_to_all | solution.py:244
  98.8 4.4 %copy-start.8 = (s32[2]{0:T(128)S(1)}, s32[2]{0:T(128)}, u32[]{:S(2)}) copy-start(s32[2]{0:T(128)} %param.7) | copy-start | bytes 28
  102.0 43.7 %collective-permute-start = (bf16[8,256,256]{2,1,0:T(8,128)(2,1)}, bf16[8,256,256]{2,1,0:T(8,128)(2,1)S(1)}, u32[]{:S(2)}, u32[]{:S(2)}) collective-permute-start(bf16[8,256,256]{2,1,0:T(8,128)(2,1)} %get-tuple-element.8), channel_id=1, source_target_pairs={{0,8},{1,9},{2,10},{3,11},{4,12},{5,13},{6,14},{7,15},{16,24},{17,... | collective-permute-start | bytes 3145736 | tf_op jit(solution)/shard_map/ppermute | solution.py:265
  145.7 1.6 copy-start.1
  147.3 1.6 copy-start.4
  155.6 63.2 %all-to-all-start.2 = ((bf16[8,256,256]{2,1,0:T(8,128)(2,1)}), bf16[8,256,256]{2,1,0:T(8,128)(2,1)S(1)}, u32[]{:S(2)}, u32[]{:S(2)}) async-start(bf16[8,256,256]{2,1,0:T(8,128)(2,1)} %shard_map.48), calls=%async_computation.2 | async-start | bytes 2097152 | tf_op jit(solution)/shard_map/all_to_all | solution.py:244
  166.7 42.3 %collective-permute-start.1 = (bf16[8,256,256]{2,1,0:T(8,128)(2,1)}, bf16[8,256,256]{2,1,0:T(8,128)(2,1)S(1)}, u32[]{:S(2)}, u32[]{:S(2)}) collective-permute-start(bf16[8,256,256]{2,1,0:T(8,128)(2,1)} %get-tuple-element.7), channel_id=1, source_target_pairs={{0,8},{1,9},{2,10},{3,11},{4,12},{5,13},{6,14},{7,15},{16,24},{17,... | collective-permute-start | bytes 3145736 | tf_op jit(solution)/shard_map/ppermute | solution.py:265
  209.0 1.6 copy-start.2
  210.6 1.6 copy-start.5
  218.9 17.4 %copy-start.6 = (bf16[8,256,256]{2,1,0:T(8,128)(2,1)}, bf16[8,256,256]{2,1,0:T(8,128)(2,1)S(1)}, u32[]{:S(2)}) copy-start(bf16[8,256,256]{2,1,0:T(8,128)(2,1)S(1)} %all-to-all-done.2.refs_0_) | copy-start | bytes 3145732
  218.9 86.6 %all-to-all-start.3 = ((bf16[8,256,256]{2,1,0:T(8,128)(2,1)}), bf16[8,256,256]{2,1,0:T(8,128)(2,1)}, u32[]{:S(2)}, u32[]{:S(2)}) async-start(bf16[8,256,256]{2,1,0:T(8,128)(2,1)} %shard_map.49), calls=%async_computation.3 | async-start | bytes 2097152 | tf_op jit(solution)/shard_map/all_to_all | solution.py:244
  236.3 41.2 %collective-permute-start.2 = (bf16[8,256,256]{2,1,0:T(8,128)(2,1)S(1)}, bf16[8,256,256]{2,1,0:T(8,128)(2,1)S(1)}, u32[]{:S(2)}, u32[]{:S(2)}) collective-permute-start(bf16[8,256,256]{2,1,0:T(8,128)(2,1)S(1)} %get-tuple-element.6), channel_id=1, source_target_pairs={{0,8},{1,9},{2,10},{3,11},{4,12},{5,13},{6,14},{7,15},{16,24},{17,... | collective-permute-start | bytes 3145736 | tf_op jit(solution)/shard_map/ppermute | solution.py:265
  305.5 17.3 %copy-start.7 = (bf16[8,256,256]{2,1,0:T(8,128)(2,1)S(1)}, bf16[8,256,256]{2,1,0:T(8,128)(2,1)}, u32[]{:S(2)}) copy-start(bf16[8,256,256]{2,1,0:T(8,128)(2,1)} %get-tuple-element.5) | copy-start | bytes 3145732
  305.5 73.2 %all-to-all-start.6 = ((bf16[8,256,256]{2,1,0:T(8,128)(2,1)}), bf16[8,256,256]{2,1,0:T(8,128)(2,1)}, u32[]{:S(2)}, u32[]{:S(2)}) async-start(bf16[8,256,256]{2,1,0:T(8,128)(2,1)} %shard_map.52), calls=%async_computation.6 | async-start | bytes 2097152 | tf_op jit(solution)/shard_map/all_to_all | solution.py:244
  322.9 28.4 %collective-permute-start.3 = (bf16[8,256,256]{2,1,0:T(8,128)(2,1)S(1)}, bf16[8,256,256]{2,1,0:T(8,128)(2,1)S(1)}, u32[]{:S(2)}, u32[]{:S(2)}) collective-permute-start(bf16[8,256,256]{2,1,0:T(8,128)(2,1)S(1)} %copy-done.7), channel_id=1, source_target_pairs={{0,8},{1,9},{2,10},{3,11},{4,12},{5,13},{6,14},{7,15},{16,24},{17,... | collective-permute-start | bytes 3145736 | tf_op jit(solution)/shard_map/ppermute | solution.py:265

commit v3 on v2

--- a/solution.py
+++ b/solution.py
@@ -19,33 +19,69 @@
 EXP_SCALE = SOFT_CAP * math.log2(math.e)
 
 
-def attend_half_kernel(
-    width, span, info_ref, query_ref, own_ref, early_ref, out_ref, key_all, value_ext, total_ref
-):
+def attend_half_kernel(phase, width, span, info_ref, query_ref, *refs):
+    refs = list(refs)
+    own_ref = refs.pop(0) if phase != "early" else None
+    early_ref = refs.pop(0) if phase != "own" else None
+    begun_ref = refs.pop(0) if phase == "early" else None
+    out_ref, key_all, value_ext, total_ref = refs
     index = pl.program_id(0)
     valid = info_ref[0]
     base = pl.multiple_of(info_ref[1], span)
-    blocks, _, rows, _ = own_ref.shape
-    part = blocks * rows
+    count = key_all.shape[0]
     start = base + index * width
+
+    def hold(at, block):
+        block = block.reshape(-1, 2 * HD)
+        key_all[pl.ds(at, block.shape[0]), :] = block[:, :HD]
+        value_ext[pl.ds(at, block.shape[0]), :HD] = block[:, HD:]
 
     @pl.when((index == 0) & (base < valid))
     def _():
-        early = early_ref[...].reshape(part, 2 * HD)
-        key_all[:part, :] = early[:, :HD]
-        value_ext[:part, :HD] = early[:, HD:]
-        own = own_ref[:, 0].reshape(part, 2 * HD)
-        key_all[pl.ds(base, part), :] = own[:, :HD]
-        value_ext[pl.ds(base, part), :HD] = own[:, HD:]
-        value_ext[:, HD:] = jnp.ones((2 * part, HD), jnp.bfloat16)
+        value_ext[:, HD:] = jnp.ones((count, HD), jnp.bfloat16)
+        if phase == "both":
+            hold(0, early_ref[...])
+            hold(base, own_ref[:, 0])
+        elif phase == "own":
+            hold(0, own_ref[:, 0])
+        else:
+            hold(0, early_ref[...])
 
     attend_block(
-        GROUP, width, span, start, valid, query_ref, (0, 0), key_all, value_ext, out_ref, (0,), total_ref
+        GROUP,
+        width,
+        span,
+        start,
+        valid,
+        query_ref,
+        (0, 0),
+        key_all,
+        value_ext,
+        out_ref,
+        (0,),
+        total_ref,
+        phase,
+        base,
+        begun_ref,
     )
 
 
 def attend_block(
-    heads, width, span, start, valid, query_ref, at_q, key_all, value_ext, out_ref, at_o, total_ref
+    heads,
+    width,
+    span,
+    start,
+    valid,
+    query_ref,
+    at_q,
+    key_all,
+    value_ext,
+    out_ref,
+    at_o,
+    total_ref,
+    phase="both",
+    base=0,
+    begun_ref=None,
 ):
     @pl.when(start >= valid)
     def _():
@@ -57,13 +93,18 @@
             [query_ref[at_q + (slice(None), slice(h * HD, (h + 1) * HD))] for h in range(heads)],
             axis=0,
         )
-        total_ref[...] = jnp.zeros_like(total_ref)
+        if phase == "early":
+            total_ref[...] = begun_ref[0]
+        else:
+            total_ref[...] = jnp.zeros_like(total_ref)
+        shift = base if phase == "own" else 0
 
         def step(block, masked):
             first = pl.multiple_of(block * span, span)
+            held = pl.ds(pl.multiple_of(first - shift, span), span)
             score = lax.dot_general(
                 block_q,
-                key_all[pl.ds(first, span), :],
+                key_all[held, :],
                 (((1,), (1,)), ((), ())),
                 preferred_element_type=jnp.float32,
             )
@@ -82,7 +123,7 @@
                 )
             total_ref[...] += jnp.dot(
                 weight.astype(jnp.bfloat16),
-                value_ext[pl.ds(first, span), :],
+                value_ext[held, :],
                 preferred_element_type=jnp.float32,
             )
 
@@ -97,8 +138,14 @@
             step(block, True)
             return carry
 
-        lax.fori_loop(0, full, plain, 0)
-        lax.fori_loop(full, stop, edge, 0)
+        if phase == "early":
+            lax.fori_loop(0, base // span, plain, 0)
+        else:
+            lax.fori_loop(shift // span, full, plain, 0)
+            lax.fori_loop(full, stop, edge, 0)
+        if phase == "own":
+            out_ref[0] = total_ref[...]
+            return
         live = start + lax.broadcasted_iota(jnp.int32, (width, HD), 0) < valid
         for h in range(heads):
             part = slice(h * width, (h + 1) * width)
@@ -108,37 +155,55 @@
             ).astype(jnp.bfloat16)
 
 
-def attend_half(query, own, early, info, which):
+def attend_half(query, own, early, begun, info, which):
     half, _, rows, size = query.shape
     part = half * rows
     span = min(512, part)
+    phase = "own" if early is None else "both" if begun is None else "early"
+    held = part if phase != "both" else 2 * part
+    specs = [pl.BlockSpec((1, 1, rows, size), lambda i, _: (i, which, 0, 0))]
+    whole = pl.BlockSpec((half, 1, rows, 2 * HD), lambda i, _: (0, 0, 0, 0))
+    sums = pl.BlockSpec((1, GROUP * rows, 2 * HD), lambda i, _: (i, 0, 0))
+    arrays = [query]
+    if phase != "early":
+        specs.append(whole)
+        arrays.append(own)
+    if phase != "own":
+        specs.append(pl.BlockSpec((half, rows, 2 * HD), lambda i, _: (0, 0, 0)))
+        arrays.append(early)
+    if phase == "early":
+        specs.append(sums)
+        arrays.append(begun)
+    if phase == "own":
+        out_spec = sums
+        out_shape = jax.ShapeDtypeStruct((half, GROUP * rows, 2 * HD), jnp.float32)
+    else:
+        out_spec = pl.BlockSpec((1, rows, size), lambda i, _: (i, 0, 0))
+        out_shape = jax.ShapeDtypeStruct((half, rows, size), jnp.bfloat16)
+    work = {"own": 2, "early": 4, "both": 6}[phase]
     return pl.pallas_call(
-        functools.partial(attend_half_kernel, rows, span),
+        functools.partial(attend_half_kernel, phase, rows, span),
         grid_spec=pltpu.PrefetchScalarGridSpec(
             num_scalar_prefetch=1,
             grid=(half,),
-            in_specs=[
-                pl.BlockSpec((1, 1, rows, size), lambda i, _: (i, which, 0, 0)),
-                pl.BlockSpec((half, 1, rows, 2 * HD), lambda i, _: (0, which, 0, 0)),
-                pl.BlockSpec((half, rows, 2 * HD), lambda i, _: (0, 0, 0)),
-            ],
-            out_specs=pl.BlockSpec((1, rows, size), lambda i, _: (i, 0, 0)),
+            in_specs=specs,
+            out_specs=out_spec,
             scratch_shapes=[
-                pltpu.VMEM((2 * part, HD), jnp.bfloat16),
-                pltpu.VMEM((2 * part, 2 * HD), jnp.bfloat16),
+                pltpu.VMEM((held, HD), jnp.bfloat16),
+                pltpu.VMEM((held, 2 * HD), jnp.bfloat16),
                 pltpu.VMEM((GROUP * rows, 2 * HD), jnp.float32),
             ],
         ),
-        out_shape=jax.ShapeDtypeStruct((half, rows, size), jnp.bfloat16),
+        out_shape=out_shape,
         cost_estimate=pl.CostEstimate(
-            flops=6 * GROUP * part * part * HD,
+            flops=work * GROUP * part * part * HD,
             bytes_accessed=2 * part * HD * 8,
             transcendentals=GROUP * part * part,
         ),
         compiler_params=pltpu.CompilerParams(
             dimension_semantics=("arbitrary",), vmem_limit_bytes=40 * 1024 * 1024
         ),
-    )(info, query, own, early)
+    )(info, *arrays)
 
 
 def attend_kernel(heads, width, span, length_ref, packed_ref, out_ref, key_all, value_ext, total_ref):
@@ -187,27 +252,29 @@
     )(valid, packed)
 
 
-def pack_kernel(take, *refs):
-    out_ref = refs[-1]
+def pack_kernel(take, owned, *refs):
+    count = len(refs) - owned
     for h in range(take):
+        out_ref = refs[count + h % owned]
         first = 0
-        for ref in refs[:-1]:
+        for ref in refs[:count]:
             size = ref.shape[2] // take
-            out_ref[h, :, first : first + size] = ref[0, :, h * size : (h + 1) * size]
+            out_ref[h // owned, :, first : first + size] = ref[0, :, h * size : (h + 1) * size]
             first += size
 
 
-def pack(arrays, s):
+def pack(arrays, s, owned):
     rows = arrays[0].shape[1]
-    take = min(4, KVH)
+    take = min(4, KVH) // owned * owned
     sizes = [a.shape[2] // KVH for a in arrays]
     total = sum(sizes)
+    shape = jax.ShapeDtypeStruct((KVH // owned, rows, total), jnp.bfloat16)
     return pl.pallas_call(
-        functools.partial(pack_kernel, take),
+        functools.partial(pack_kernel, take, owned),
         grid=(KVH // take,),
         in_specs=[pl.BlockSpec((1, rows, take * size), lambda h: (s, 0, h)) for size in sizes],
-        out_specs=pl.BlockSpec((take, rows, total), lambda h: (h, 0, 0)),
-        out_shape=jax.ShapeDtypeStruct((KVH, rows, total), jnp.bfloat16),
+        out_specs=[pl.BlockSpec((take // owned, rows, total), lambda h: (h, 0, 0))] * owned,
+        out_shape=[shape] * owned,
         cost_estimate=pl.CostEstimate(
             flops=0, bytes_accessed=4 * KVH * rows * total, transcendentals=0
         ),
@@ -216,22 +283,24 @@
 
 def unpack_kernel(take, owned, *refs):
     out_ref = refs[-1]
-    size = refs[0].shape[2]
+    size = refs[0].shape[3]
     for d in range(take):
         for n, ref in enumerate(refs[:-1]):
             s, o = n // owned, n % owned
             first = (d * owned + o) * size
-            out_ref[s, :, first : first + size] = ref[d]
-
-
-def unpack(returned, owned):
-    half, rows, size = returned[0].shape
+            out_ref[s, :, first : first + size] = ref[d, 0]
+
+
+def unpack(returned, places, owned):
+    half, _, rows, size = returned[0].shape
     seqs = len(returned) // owned
     take = min(2, half)
     return pl.pallas_call(
         functools.partial(unpack_kernel, take, owned),
         grid=(half // take,),
-        in_specs=[pl.BlockSpec((take, rows, size), lambda d: (d, 0, 0))] * len(returned),
+        in_specs=[
+            pl.BlockSpec((take, 1, rows, size), lambda d, o=o: (d, o, 0, 0)) for o in places
+        ],
         out_specs=pl.BlockSpec((seqs, rows, take * owned * size), lambda d: (0, 0, d)),
         out_shape=jax.ShapeDtypeStruct((seqs, rows, half * owned * size), jnp.bfloat16),
         cost_estimate=pl.CostEstimate(
@@ -256,23 +325,32 @@
     base = jnp.where(lax.axis_index("tp") >= half, half * rows, 0).astype(jnp.int32)
     held = []
     for s in range(seqs):
-        packed = pack((keys, values), s).reshape(half, owned * rows, -1)
-        pair = exchange(packed, groups)
-        pair = pair.reshape(half, owned, rows, -1)
-        early = []
+        pairs, early = [], []
+        for o, packed in enumerate(pack((keys, values), s, owned)):
+            pairs.append(exchange(packed, groups))
+            early.append(lax.ppermute(pairs[o], "tp", forward))
+        packed = pack((queries,), s, 1)[0].reshape(half, owned * rows, -1)
+        query = exchange(packed, groups)
+        held.append((query.reshape(half, owned, rows, -1), pairs, early))
+    returned, places = [], []
+    for s in range(seqs):
+        query, pairs, early = held[s]
+        info = jnp.stack([lengths[s], base])
+        outs = []
         for o in range(owned):
-            part = pair[:, o]
-            early.append(lax.ppermute(part, "tp", forward))
-        packed = pack((queries,), s).reshape(half, owned * rows, -1)
-        query = exchange(packed, groups)
-        held.append((query.reshape(half, owned, rows, -1), pair, early))
-    returned = []
-    for s in range(seqs):
-        query, pair, early = held[s]
-        info = jnp.stack([lengths[s], base])
-        for o in range(owned):
-            returned.append(exchange(attend_half(query, pair, early[o], info, o), groups))
-    return unpack(returned, owned)
+            pair, begun = pairs[o][:, None], None
+            if s == seqs - 1 and o == owned - 1:
+                begun = attend_half(query, pair, None, None, info, o)
+            outs.append(attend_half(query, pair, early[o], begun, info, o))
+        if s < seqs - 1:
+            output = jnp.stack(outs, axis=1).reshape(half, owned * rows, -1)
+            back = exchange(output, groups).reshape(half, owned, rows, -1)
+            returned += [back] * owned
+            places += range(owned)
+        else:
+            returned += [exchange(output, groups)[:, None] for output in outs]
+            places += [0] * owned
+    return unpack(returned, places, owned)
 
 
 def halves_fit(devices):

time: 426 us -> 394 us (0.925)
  the two profiles are of different devices: /device:TPU:18 before, /device:TPU:2 now
where the time goes in v3:
time: 394 us; the launch traced here: 393 us
  starting transfers between devices  118 us (30%)
  waiting for transfers between devices  95 us (24%)
  blocking collectives  89.8 us (23%)
  Pallas kernels  76.3 us (19%)
  local copies, waits for them, and re-layouts  11.9 us (3%)
    all_to_all x3, blocking collectives, exchange(): lax.all_to_all(array, 'tp', split_axis=0, concat_axis=0, tiled=True, axis...  89.8 us
    all_to_all x6, starting transfers between devices, exchange(): lax.all_to_all(array, 'tp', split_axis=0, concat_axis=0, tiled=True, axis...  70.8 us
    pallas_call x5, Pallas kernels, attend_half(): pl.pallas_call(functools.partial(attend_half_kernel, phase, rows, span),...  56.2 us
    ppermute x4, waiting for transfers between devices, by_halves(): early.append(lax.ppermute(pairs[o], 'tp', forward))  52.1 us
    ppermute x4, starting transfers between devices, by_halves(): early.append(lax.ppermute(pairs[o], 'tp', forward))  47.1 us
    all_to_all x6, waiting for transfers between devices, exchange(): lax.all_to_all(array, 'tp', split_axis=0, concat_axis=0, tiled=True, axis...  43 us
    pallas_call x4, Pallas kernels, pack(): pl.pallas_call(functools.partial(pack_kernel, take, owned), grid=(KVH //...  15.4 us
    unnamed x20, local copies, waits for them, and re-layouts  11.1 us
  transfers between devices with their start and end apart: 10, of which 6 were waited for; matrix products, arithmetic and copies ran while one was open for 1% of the time, Pallas kernels for 17%

profile of v3, /device:TPU:2, one launch (start us, length us, event | category | flops | bytes accessed | tf_op | source)
XLA Modules:
  0.0 392.7 jit_solution(4770716799204331662)
XLA Ops:
  0.0 3.9 shard_map.47
  3.9 18.8 %all_to_all.45 = bf16[8,256,256]{2,1,0:T(8,128)(2,1)} all-to-all(bf16[8,256,256]{2,1,0:T(8,128)(2,1)} %get-tuple-element.10), channel_id=1, replica_groups={{0,1,2,3,4,5,6,7},{8,9,10,11,12,13,14,15},{16,17,18,19,20,21,22,23},{24..., dimensions={0} | all-to-all | bytes 2097152 | tf_op jit(solution)/shard_map/all_to_all | solution.py:313
  22.7 3.6 all-to-all-start.1
  26.3 3.9 shard_map.51
  30.2 10.5 %all-to-all-done.1 = bf16[8,256,256]{2,1,0:T(8,128)(2,1)S(1)} async-done(((bf16[8,256,256]{2,1,0:T(8,128)(2,1)}), bf16[8,256,256]{2,1,0:T(8,128)(2,1)S(1)}, u32[]{:S(2)}, u32[]{:S(2)}) %all-to-all-start.1) | async-done | bytes 1048608 | tf_op jit(solution)/shard_map/all_to_all | solution.py:313
  40.7 18.9 %all_to_all.46 = bf16[8,256,256]{2,1,0:T(8,128)(2,1)} all-to-all(bf16[8,256,256]{2,1,0:T(8,128)(2,1)} %get-tuple-element.11), channel_id=1, replica_groups={{0,1,2,3,4,5,6,7},{8,9,10,11,12,13,14,15},{16,17,18,19,20,21,22,23},{24..., dimensions={0} | all-to-all | bytes 2097152 | tf_op jit(solution)/shard_map/all_to_all | solution.py:313
  59.6 3.6 all-to-all-start.7
  63.1 3.8 shard_map.50
  66.9 10.6 %all-to-all-done.7 = bf16[8,256,256]{2,1,0:T(8,128)(2,1)S(1)} async-done(((bf16[8,256,256]{2,1,0:T(8,128)(2,1)}), bf16[8,256,256]{2,1,0:T(8,128)(2,1)S(1)}, u32[]{:S(2)}, u32[]{:S(2)}) %all-to-all-start.7) | async-done | bytes 1048608 | tf_op jit(solution)/shard_map/all_to_all | solution.py:313
  77.5 1.0 copy-done.4
  78.5 3.6 all-to-all-start.4
  82.1 3.8 shard_map.46
  85.9 21.9 %all-to-all-done.4 = bf16[8,512,256]{2,1,0:T(8,128)(2,1)S(1)} async-done(((bf16[8,512,256]{2,1,0:T(8,128)(2,1)}), bf16[8,512,256]{2,1,0:T(8,128)(2,1)S(1)}, u32[]{:S(2)}, u32[]{:S(2)}) %all-to-all-start.4) | async-done | bytes 2097184 | tf_op jit(solution)/shard_map/all_to_all | solution.py:313
  107.7 1.3 copy-done
  109.1 3.7 all-to-all-start
  112.8 5.5 %collective-permute-start.2 = (bf16[8,256,256]{2,1,0:T(8,128)(2,1)}, bf16[8,256,256]{2,1,0:T(8,128)(2,1)}, u32[]{:S(2)}, u32[]{:S(2)}) collective-permute-start(bf16[8,256,256]{2,1,0:T(8,128)(2,1)} %all_to_all.46), channel_id=1, source_target_pairs={{0,8},{1,9},{2,10},{3,11},{4,12},{5,13},{6,14},{7,15},{16,24},{17,... | collective-permute-start | bytes 3145736 | tf_op jit(solution)/shard_map/ppermute | solution.py:331
  118.3 0.6 fusion
  118.9 0.7 pad_add_fusion.1.info_ref
  119.7 39.3 %collective-permute-done.2.refs_1_ = bf16[8,256,256]{2,1,0:T(8,128)(2,1)} collective-permute-done((bf16[8,256,256]{2,1,0:T(8,128)(2,1)}, bf16[8,256,256]{2,1,0:T(8,128)(2,1)}, u32[]{:S(2)}, u32[]{:S(2)}) %collective-permute-start.2) | collective-permute-done | bytes 1048608 | tf_op jit(solution)/shard_map/ppermute | solution.py:331
  159.0 1.6 copy-done.1
  160.6 1.2 copy-done.6
  161.8 14.3 %shard_map.52 = bf16[8,256,256]{2,1,0:T(8,128)(2,1)S(1)} custom-call(s32[2]{0:T(128)S(1)} %pad_add_fusion.1.info_ref, bf16[8,2,256,256]{3,2,1,0:T(8,128)(2,1)S(1)} %bitcast.25, bf16[8,1,256,256]{3,2,1,0:T(8,128)(2,1)S(1)} %bitcast.31, bf16[8,256,256]{2,1,0:T(8,128)(2,1)} %collective-permute-done.2.refs_1_), custom_call_target="tpu_custom_call" | custom-call | flops 6442450944 | bytes 4194304 | tf_op jit(solution)/shard_map/pallas_call | solution.py:184
  176.1 1.0 copy-done.8
  177.1 0.0 all-to-all-done
  177.1 8.0 %all-to-all-start.6 = ((bf16[8,256,256]{2,1,0:T(8,128)(2,1)}), bf16[8,256,256]{2,1,0:T(8,128)(2,1)}, u32[]{:S(2)}, u32[]{:S(2)}) async-start(bf16[8,256,256]{2,1,0:T(8,128)(2,1)} %copy-done.8), calls=%async_computation.6 | async-start | bytes 2097152 | tf_op jit(solution)/shard_map/all_to_all | solution.py:313
  185.1 18.6 %collective-permute-start.3 = (bf16[8,256,256]{2,1,0:T(8,128)(2,1)}, bf16[8,256,256]{2,1,0:T(8,128)(2,1)S(1)}, u32[]{:S(2)}, u32[]{:S(2)}) collective-permute-start(bf16[8,256,256]{2,1,0:T(8,128)(2,1)} %copy-done.4), channel_id=1, source_target_pairs={{0,8},{1,9},{2,10},{3,11},{4,12},{5,13},{6,14},{7,15},{16,24},{17,... | collective-permute-start | bytes 3145736 | tf_op jit(solution)/shard_map/ppermute | solution.py:331
  203.7 2.3 collective-permute-start.1
  206.0 1.6 copy-done.2
  207.6 1.2 copy-done.5
  208.8 12.7 %shard_map.53.refs_1_ = f32[8,512,256]{2,1,0:T(8,128)S(1)} custom-call(s32[2]{0:T(128)S(1)} %pad_add_fusion.1.info_ref, bf16[8,2,256,256]{3,2,1,0:T(8,128)(2,1)S(1)} %bitcast.26, bf16[8,1,256,256]{3,2,1,0:T(8,128)(2,1)S(1)} %bitcast.30), custom_call_target="tpu_custom_call" | custom-call | flops 2147483648 | bytes 4194304 | tf_op jit(solution)/shard_map/pallas_call | solution.py:184
  221.5 6.0 %collective-permute-done.3.refs_0_ = bf16[8,256,256]{2,1,0:T(8,128)(2,1)S(1)} collective-permute-done((bf16[8,256,256]{2,1,0:T(8,128)(2,1)}, bf16[8,256,256]{2,1,0:T(8,128)(2,1)S(1)}, u32[]{:S(2)}, u32[]{:S(2)}) %collective-permute-start.3) | collective-permute-done | bytes 1048608 | tf_op jit(solution)/shard_map/ppermute | solution.py:331
  227.5 1.7 shard_map.54
  229.2 0.0 copy-start.7
  229.3 1.0 copy-done.7
  230.2 0.0 all-to-all-done.6
  230.2 48.3 %all-to-all-start.8 = ((bf16[8,256,256]{2,1,0:T(8,128)(2,1)}), bf16[8,256,256]{2,1,0:T(8,128)(2,1)}, u32[]{:S(2)}, u32[]{:S(2)}) async-start(bf16[8,256,256]{2,1,0:T(8,128)(2,1)} %copy-done.7), calls=%async_computation.8 | async-start | bytes 2097152 | tf_op jit(solution)/shard_map/all_to_all | solution.py:313
  278.5 20.7 %collective-permute-start = (bf16[8,256,256]{2,1,0:T(8,128)(2,1)S(1)}, bf16[8,256,256]{2,1,0:T(8,128)(2,1)S(1)}, u32[]{:S(2)}, u32[]{:S(2)}) collective-permute-start(bf16[8,256,256]{2,1,0:T(8,128)(2,1)S(1)} %all-to-all-done.1), channel_id=1, source_target_pairs={{0,8},{1,9},{2,10},{3,11},{4,12},{5,13},{6,14},{7,15},{16,24},{17,... | collective-permute-start | bytes 3145736 | tf_op jit(solution)/shard_map/ppermute | solution.py:331
  299.3 0.7 pad_add_fusion.info_ref
  299.9 0.0 collective-permute-done.1.refs_1_
  300.0 1.2 copy-done.3
  301.2 14.3 %shard_map.49 = bf16[8,256,256]{2,1,0:T(8,128)(2,1)S(1)} custom-call(s32[2]{0:T(128)S(1)} %pad_add_fusion.info_ref, bf16[8,2,256,256]{3,2,1,0:T(8,128)(2,1)S(1)} %bitcast.23, bf16[8,1,256,256]{3,2,1,0:T(8,128)(2,1)S(1)} %bitcast.29, bf16[8,256,256]{2,1,0:T(8,128)(2,1)} %collective-permute-done.1.refs_1_), custom_call_target="tpu_custom_call" | custom-call | flops 6442450944 | bytes 4194304 | tf_op jit(solution)/shard_map/pallas_call | solution.py:184
  315.5 6.8 %collective-permute-done.refs_1_ = bf16[8,256,256]{2,1,0:T(8,128)(2,1)S(1)} collective-permute-done((bf16[8,256,256]{2,1,0:T(8,128)(2,1)S(1)}, bf16[8,256,256]{2,1,0:T(8,128)(2,1)S(1)}, u32[]{:S(2)}, u32[]{:S(2)}) %collective-permute-start) | collective-permute-done | bytes 1048608 | tf_op jit(solution)/shard_map/ppermute | solution.py:331
  322.3 13.1 %shard_map.48 = bf16[8,256,256]{2,1,0:T(8,128)(2,1)S(1)} custom-call(s32[2]{0:T(128)S(1)} %pad_add_fusion.info_ref, bf16[8,2,256,256]{3,2,1,0:T(8,128)(2,1)S(1)} %bitcast.24, bf16[8,1,256,256]{3,2,1,0:T(8,128)(2,1)S(1)} %bitcast.28, bf16[8,256,256]{2,1,0:T(8,128)(2,1)S(1)} %collective-permute-done.refs_1_), custom_call_target="tpu_custom_call" | custom-call | flops 6442450944 | bytes 4194304 | tf_op jit(solution)/shard_map/pallas_call | solution.py:184
  335.4 0.2 pad_maximum_fusion
  335.6 0.1 copy.11
  335.8 0.0 all-to-all-done.8
  335.8 52.1 %all_to_all.47 = bf16[8,512,256]{2,1,0:T(8,128)(2,1)} all-to-all(bf16[8,512,256]{2,1,0:T(8,128)(2,1)S(1)} %bitcast.38), channel_id=1, replica_groups={{0,1,2,3,4,5,6,7},{8,9,10,11,12,13,14,15},{16,17,18,19,20,21,22,23},{24..., dimensions={0} | all-to-all | bytes 4194304 | tf_op jit(solution)/shard_map/all_to_all | solution.py:313
  387.9 4.8 %shard_map.55 = bf16[2,256,4096]{2,1,0:T(8,128)(2,1)} custom-call(bf16[8,2,256,256]{3,2,1,0:T(8,128)(2,1)} %bitcast.34, bf16[8,2,256,256]{3,2,1,0:T(8,128)(2,1)} %bitcast.35, bf16[8,1,256,256]{3,2,1,0:T(8,128)(2,1)} %bitcast.15.refs_2_, bf16[8,1,256,256]{3,2,1,0:T(8,128)(2,1)} %bitcast.18.refs_3_), custom_call_target="tpu_custom_call" | custom-call | bytes 8388608 | tf_op jit(solution)/shard_map/pallas_call | solution.py:298
  (10 shorter events, 0.0 us)
Async XLA Ops:
  22.7 18.0 %all-to-all-start.1 = ((bf16[8,256,256]{2,1,0:T(8,128)(2,1)}), bf16[8,256,256]{2,1,0:T(8,128)(2,1)S(1)}, u32[]{:S(2)}, u32[]{:S(2)}) async-start(bf16[8,256,256]{2,1,0:T(8,128)(2,1)} %get-tuple-element.9), calls=%async_computation.1 | async-start | bytes 2097152 | tf_op jit(solution)/shard_map/all_to_all | solution.py:313
  59.6 18.0 %all-to-all-start.7 = ((bf16[8,256,256]{2,1,0:T(8,128)(2,1)}), bf16[8,256,256]{2,1,0:T(8,128)(2,1)S(1)}, u32[]{:S(2)}, u32[]{:S(2)}) async-start(bf16[8,256,256]{2,1,0:T(8,128)(2,1)} %get-tuple-element.12), calls=%async_computation.7 | async-start | bytes 2097152 | tf_op jit(solution)/shard_map/all_to_all | solution.py:313
  77.5 1.0 copy-start.4
  78.5 29.2 %all-to-all-start.4 = ((bf16[8,512,256]{2,1,0:T(8,128)(2,1)}), bf16[8,512,256]{2,1,0:T(8,128)(2,1)S(1)}, u32[]{:S(2)}, u32[]{:S(2)}) async-start(bf16[8,512,256]{2,1,0:T(8,128)(2,1)} %bitcast.37), calls=%async_computation.4 | async-start | bytes 4194304 | tf_op jit(solution)/shard_map/all_to_all | solution.py:313
  107.7 1.3 copy-start
  109.1 9.2 %copy-start.9 = (s32[2]{0:T(128)S(1)}, s32[2]{0:T(128)}, u32[]{:S(2)}) copy-start(s32[2]{0:T(128)} %param.7) | copy-start | bytes 28
  109.1 68.0 %all-to-all-start = ((bf16[8,512,256]{2,1,0:T(8,128)(2,1)}), bf16[8,512,256]{2,1,0:T(8,128)(2,1)S(1)}, u32[]{:S(2)}, u32[]{:S(2)}) async-start(bf16[8,512,256]{2,1,0:T(8,128)(2,1)} %bitcast.36), calls=%async_computation | async-start | bytes 4194304 | tf_op jit(solution)/shard_map/all_to_all | solution.py:313
  112.8 46.1 %collective-permute-start.2 = (bf16[8,256,256]{2,1,0:T(8,128)(2,1)}, bf16[8,256,256]{2,1,0:T(8,128)(2,1)}, u32[]{:S(2)}, u32[]{:S(2)}) collective-permute-start(bf16[8,256,256]{2,1,0:T(8,128)(2,1)} %all_to_all.46), channel_id=1, source_target_pairs={{0,8},{1,9},{2,10},{3,11},{4,12},{5,13},{6,14},{7,15},{16,24},{17,... | collective-permute-start | bytes 3145736 | tf_op jit(solution)/shard_map/ppermute | solution.py:331
  159.0 1.6 copy-start.1
  160.6 1.2 copy-start.6
  176.1 1.0 copy-start.8
  177.1 53.1 %all-to-all-start.6 = ((bf16[8,256,256]{2,1,0:T(8,128)(2,1)}), bf16[8,256,256]{2,1,0:T(8,128)(2,1)}, u32[]{:S(2)}, u32[]{:S(2)}) async-start(bf16[8,256,256]{2,1,0:T(8,128)(2,1)} %copy-done.8), calls=%async_computation.6 | async-start | bytes 2097152 | tf_op jit(solution)/shard_map/all_to_all | solution.py:313
  185.1 42.4 %collective-permute-start.3 = (bf16[8,256,256]{2,1,0:T(8,128)(2,1)}, bf16[8,256,256]{2,1,0:T(8,128)(2,1)S(1)}, u32[]{:S(2)}, u32[]{:S(2)}) collective-permute-start(bf16[8,256,256]{2,1,0:T(8,128)(2,1)} %copy-done.4), channel_id=1, source_target_pairs={{0,8},{1,9},{2,10},{3,11},{4,12},{5,13},{6,14},{7,15},{16,24},{17,... | collective-permute-start | bytes 3145736 | tf_op jit(solution)/shard_map/ppermute | solution.py:331
  203.7 96.2 %collective-permute-start.1 = (bf16[8,256,256]{2,1,0:T(8,128)(2,1)}, bf16[8,256,256]{2,1,0:T(8,128)(2,1)}, u32[]{:S(2)}, u32[]{:S(2)}) collective-permute-start(bf16[8,256,256]{2,1,0:T(8,128)(2,1)} %all_to_all.45), channel_id=1, source_target_pairs={{0,8},{1,9},{2,10},{3,11},{4,12},{5,13},{6,14},{7,15},{16,24},{17,... | collective-permute-start | bytes 3145736 | tf_op jit(solution)/shard_map/ppermute | solution.py:331
  206.0 1.6 copy-start.2
  207.6 1.2 copy-start.5
  229.2 1.0 copy-start.7
  230.2 105.6 %all-to-all-start.8 = ((bf16[8,256,256]{2,1,0:T(8,128)(2,1)}), bf16[8,256,256]{2,1,0:T(8,128)(2,1)}, u32[]{:S(2)}, u32[]{:S(2)}) async-start(bf16[8,256,256]{2,1,0:T(8,128)(2,1)} %copy-done.7), calls=%async_computation.8 | async-start | bytes 2097152 | tf_op jit(solution)/shard_map/all_to_all | solution.py:313
  278.5 43.8 %collective-permute-start = (bf16[8,256,256]{2,1,0:T(8,128)(2,1)S(1)}, bf16[8,256,256]{2,1,0:T(8,128)(2,1)S(1)}, u32[]{:S(2)}, u32[]{:S(2)}) collective-permute-start(bf16[8,256,256]{2,1,0:T(8,128)(2,1)S(1)} %all-to-all-done.1), channel_id=1, source_target_pairs={{0,8},{1,9},{2,10},{3,11},{4,12},{5,13},{6,14},{7,15},{16,24},{17,... | collective-permute-start | bytes 3145736 | tf_op jit(solution)/shard_map/ppermute | solution.py:331
  299.9 1.2 copy-start.3
